TPU v7x, 32 devices: a whole 2x2x4 slice. The times are simulated.
32 devices in a mesh: py: 4 (over y, core), pz: 8 (over z, x).
Axes of the slice: x: 2, y: 2, z: 4, core: 2. Of those that a mesh axis runs over, the one named last changes fastest.
Arguments:
- wavefunctions: float32 [2, 8, 128, 128, 128], P(None, None, 'pz', 'py'), may hold values from -6 to 6
- potential: float32 [128, 128, 128], P('pz', 'py'), may hold values from -4 to 4
- cutoff_sq: int32 [1], replicated, may hold values from 2304 to 4096
- locked_mask: int32 [8], replicated, may hold values 0 or 1
Outputs:
- applied: float32 [2, 8, 128, 128, 128], P(None, None, 'pz', 'py')
- rayleigh: float32 [8], replicated
- residual_norm: float32 [8], replicated
All inputs are finite; a program needn't handle non-finite values.
Results may differ from a plain program's by a relative error of at most 0.00005.
Values sent between devices are 32-bit elements; how exact they have to be, the bound alone decides.
No kernel may reach another device: no remote copies, remote signals or barrier semaphores. Data moves between devices by JAX's collectives and lax.ppermute only.
A program may use at most 64 MiB of HBM per device.

v0:
```python
import math

import jax
import jax.numpy as jnp
from jax import lax
from jax.sharding import PartitionSpec as P


def make_tables(length, inverse):
    counter = jnp.arange(length, dtype=jnp.int32)
    phase = counter[:, None] * counter[None, :] % length
    angle = 2.0 * math.pi / length * phase.astype(jnp.float32)
    if inverse:
        return (jnp.cos(angle) / length, jnp.sin(angle) / length)
    return (jnp.cos(angle), -jnp.sin(angle))


def transform_axis(field, axis, tables):
    cosines, sines = tables
    letters = "abcdefgh"[: field.ndim - 1]
    place = axis - 1
    source = letters[:place] + "n" + letters[place + 1 :]
    target = letters[:place] + "k" + letters[place + 1 :]
    form = source + ",kn->" + target
    real_part = field[0]
    imag_part = field[1]
    high = lax.Precision.HIGHEST
    out_real = jnp.einsum(form, real_part, cosines, precision=high) - jnp.einsum(
        form, imag_part, sines, precision=high
    )
    out_imag = jnp.einsum(form, real_part, sines, precision=high) + jnp.einsum(
        form, imag_part, cosines, precision=high
    )
    return jnp.stack([out_real, out_imag])


def signed_square(counter, length):
    signed = jnp.where(counter < length // 2, counter, counter - length)
    return signed * signed


def kinetic_table(first_sq, second_sq, third_sq, cutoff_sq, length):
    total = first_sq[:, None, None] + second_sq[None, :, None] + third_sq[None, None, :]
    keep = (total <= cutoff_sq[0]).astype(jnp.float32)
    return 0.5 * (math.pi / length) ** 2 * total.astype(jnp.float32) * keep


def slab_kinetic(field, cutoff_sq, forward, inverse):
    parts, bands, rows_z, rows_y, length = field.shape
    size_y = lax.axis_size("py")
    size_z = lax.axis_size("pz")
    along_x = transform_axis(field, 4, forward)
    flat = jnp.moveaxis(along_x, 1, 3).reshape(parts, rows_z, rows_y, bands * length)
    planes = lax.all_to_all(
        lax.all_to_all(flat, "py", split_axis=3, concat_axis=2, tiled=True),
        "pz",
        split_axis=3,
        concat_axis=1,
        tiled=True,
    )
    width = planes.shape[3]
    start = lax.axis_index("py") * (bands * length // size_y) + lax.axis_index("pz") * width
    column = start + jnp.arange(width, dtype=jnp.int32)
    full_counter = jnp.arange(length, dtype=jnp.int32)
    full_sq = signed_square(full_counter, length)
    kinetic = kinetic_table(
        full_sq, full_sq, signed_square(column % length, length), cutoff_sq, length
    )
    spectrum = transform_axis(transform_axis(planes, 1, forward), 2, forward) * kinetic
    spatial = transform_axis(transform_axis(spectrum, 2, inverse), 1, inverse)
    returned = lax.all_to_all(
        lax.all_to_all(spatial, "py", split_axis=2, concat_axis=3, tiled=True),
        "pz",
        split_axis=1,
        concat_axis=3,
        tiled=True,
    )
    ordered = returned.reshape(parts, rows_z, rows_y, size_z, size_y, width)
    ordered = jnp.swapaxes(ordered, 3, 4).reshape(parts, rows_z, rows_y, bands, length)
    return transform_axis(jnp.moveaxis(ordered, 3, 1), 4, inverse)


def apply_kinetic(field, cutoff_sq, forward, inverse):
    return slab_kinetic(field, cutoff_sq, forward, inverse)


def body(wavefunctions, potential, cutoff_sq, locked_mask):
    length = wavefunctions.shape[4]
    forward = make_tables(length, False)
    inverse = make_tables(length, True)
    blocks = wavefunctions.shape[1] // 4

    def one_block(block, result):
        piece = lax.dynamic_slice_in_dim(wavefunctions, block * 4, 4, 1)
        done = apply_kinetic(piece, cutoff_sq, forward, inverse)
        return lax.dynamic_update_slice_in_dim(result, done, block * 4, 1)

    kinetic_part = lax.fori_loop(0, blocks, one_block, jnp.zeros_like(wavefunctions))
    applied = kinetic_part + potential[None, None] * wavefunctions
    norm_local = jnp.sum(wavefunctions * wavefunctions, axis=(0, 2, 3, 4))
    correlation_local = jnp.sum(wavefunctions * applied, axis=(0, 2, 3, 4))
    norm_sq, correlation = lax.psum((norm_local, correlation_local), ("py", "pz"))
    rayleigh = correlation / norm_sq
    residual = applied - rayleigh[None, :, None, None, None] * wavefunctions
    residual_sq = lax.psum(jnp.sum(residual * residual, axis=(0, 2, 3, 4)), ("py", "pz"))
    residual_norm = jnp.sqrt(residual_sq / norm_sq) * (1.0 - locked_mask.astype(jnp.float32))
    return (applied, rayleigh, residual_norm)


def solution(mesh):
    in_specs = (P(None, None, "pz", "py", None), P("pz", "py", None), P(), P())
    out_specs = (P(None, None, "pz", "py", None), P(), P())
    return jax.shard_map(body, mesh=mesh, in_specs=in_specs, out_specs=out_specs, check_vma=False)
```

profile of v0, /device:TPU:0, one launch (start us, length us, event | category | flops | bytes accessed | tf_op | source)
XLA Modules:
  0.0 693.6 jit_solution(16688748125790381216)
XLA Ops:
  3.2 599.9 %while.18 = (s32[]{:T(128)}, f32[2,8,16,32,128]{4,3,2,1,0:T(8,128)}, f32[2,8,16,32,128]{4,3,2,1,0:T(8,128)}, s32[1]{0:T(128)}, s32[]{:T(128)}, /*index=5*/s32[]{...) while((s32[]{:T(128)}, ...), condition=%wide.region_1.2_spmd.clone.clone, body=%wide.region_0.1_spmd.clone.clone.sunk | while | flops 9676570624 | bytes 232916592 | solution.py:98
  13.3 7.5 %copy.142 = f32[2,16,32,4,128]{2,1,0,4,3:T(8,128)} copy(f32[2,16,32,4,128]{4,2,1,3,0:T(8,128)S(1)} %maximum_bitcast_fusion.2) | data formatting | bytes 4194304 | tf_op jit(solution)/shard_map/while/body/eval_jaxpr/reshape | solution.py:53
  26.9 30.2 %all_to_all.204 = f32[4,1,131072]{2,1,0:T(1,128)} all-to-all(f32[4,1,131072]{2,1,0:T(1,128)S(1)} %reshape.143), channel_id=1, replica_groups=mesh['py'=4,'pz'=8] {'py'}, dimensions={0} | all-to-all | bytes 4194304 | tf_op jit(solution)/shard_map/while/body/eval_jaxpr/all_to_all | solution.py:55
  57.6 7.7 %reduce.4 = f32[4,131072]{1,0:T(4,128)S(1)} reduce(f32[4,1,131072]{2,1,0:T(1,128)} %all_to_all.204, f32[]{:T(128)} %broadcast.656), dimensions={1}, to_apply=%all_to_all.178.reduce_sub_computation | reduce | bytes 4194308 | tf_op jit(solution)/shard_map/while/body/eval_jaxpr/all_to_all | solution.py:55
  81.3 6.9 all-to-all-start.1
  89.3 46.3 %all-to-all-done.1 = f32[2,16,128,128]{2,1,0,3:T(8,128)S(1)} async-done(((f32[2,16,128,128]{2,1,0,3:T(8,128)}), f32[2,16,128,128]{2,1,0,3:T(8,128)S(1)}, u32[]{:S(2)}, u32[]{:S(2)}) %all-to-all-start.1) | async-done | bytes 2097184 | tf_op jit(solution)/shard_map/while/body/eval_jaxpr/all_to_all | solution.py:54
  170.9 28.1 %all_to_all.205 = f32[2,128,128,16]{1,3,0,2:T(8,128)S(1)} all-to-all(f32[2,128,128,16]{1,3,0,2:T(8,128)S(1)} %copy.151), channel_id=1, replica_groups=mesh['py'=4,'pz'=8] {'py'}, dimensions={2} | all-to-all | bytes 4194304 | tf_op jit(solution)/shard_map/while/body/eval_jaxpr/all_to_all | solution.py:72
  203.8 7.2 %reshape.145 = f32[8,1,65536]{2,1,0:T(1,128)} reshape(f32[128,2,32,64]{3,2,1,0:T(8,128)} %bitcast.327) | data formatting | bytes 4194304 | tf_op jit(solution)/shard_map/while
  214.9 48.0 %all-to-all-done.3 = f32[8,1,65536]{2,1,0:T(1,128)S(1)} async-done(((f32[8,1,65536]{2,1,0:T(1,128)}), f32[8,1,65536]{2,1,0:T(1,128)S(1)}, u32[]{:S(2)}, u32[]{:S(2)}) %all-to-all-start.3) | async-done | bytes 2097184 | tf_op jit(solution)/shard_map/while/body/eval_jaxpr/all_to_all | solution.py:71
  264.8 7.2 %reduce.5 = f32[8,65536]{1,0:T(8,128)S(1)} reduce(f32[8,1,65536]{2,1,0:T(1,128)} %copy-done, f32[]{:T(128)} %broadcast.657), dimensions={1}, to_apply=%all_to_all.189.reduce_sub_computation | reduce | bytes 4194308 | tf_op jit(solution)/shard_map/while/body/eval_jaxpr/all_to_all | solution.py:71
  275.6 7.0 %copy.154 = f32[2,16,32,8,64]{2,4,3,1,0:T(8,128)} copy(f32[2,16,32,8,64]{4,2,0,1,3:T(8,128)} %bitcast.326) | data formatting | bytes 4194304 | tf_op jit(solution)/shard_map/while/body/eval_jaxpr/all_to_all | solution.py:71
  282.6 7.9 %copy.155 = f32[2,16,32,4,8,16]{2,5,4,3,1,0:T(8,128)} copy(f32[2,16,32,4,8,16]{2,5,3,4,1,0:T(8,128)} %bitcast.320) | data formatting | bytes 4194304 | tf_op jit(solution)/shard_map/while/body/eval_jaxpr/transpose | solution.py:79
  313.5 7.5 %copy.142 = f32[2,16,32,4,128]{2,1,0,4,3:T(8,128)} copy(f32[2,16,32,4,128]{4,2,1,3,0:T(8,128)S(1)} %maximum_bitcast_fusion.2) | data formatting | bytes 4194304 | tf_op jit(solution)/shard_map/while/body/eval_jaxpr/reshape | solution.py:53
  327.2 29.1 %all_to_all.204 = f32[4,1,131072]{2,1,0:T(1,128)} all-to-all(f32[4,1,131072]{2,1,0:T(1,128)S(1)} %reshape.143), channel_id=1, replica_groups=mesh['py'=4,'pz'=8] {'py'}, dimensions={0} | all-to-all | bytes 4194304 | tf_op jit(solution)/shard_map/while/body/eval_jaxpr/all_to_all | solution.py:55
  356.8 7.7 %reduce.4 = f32[4,131072]{1,0:T(4,128)S(1)} reduce(f32[4,1,131072]{2,1,0:T(1,128)} %all_to_all.204, f32[]{:T(128)} %broadcast.656), dimensions={1}, to_apply=%all_to_all.178.reduce_sub_computation | reduce | bytes 4194308 | tf_op jit(solution)/shard_map/while/body/eval_jaxpr/all_to_all | solution.py:55
  385.6 46.7 %all-to-all-done.1 = f32[2,16,128,128]{2,1,0,3:T(8,128)S(1)} async-done(((f32[2,16,128,128]{2,1,0,3:T(8,128)}), f32[2,16,128,128]{2,1,0,3:T(8,128)S(1)}, u32[]{:S(2)}, u32[]{:S(2)}) %all-to-all-start.1) | async-done | bytes 2097184 | tf_op jit(solution)/shard_map/while/body/eval_jaxpr/all_to_all | solution.py:54
  467.6 28.1 %all_to_all.205 = f32[2,128,128,16]{1,3,0,2:T(8,128)S(1)} all-to-all(f32[2,128,128,16]{1,3,0,2:T(8,128)S(1)} %copy.151), channel_id=1, replica_groups=mesh['py'=4,'pz'=8] {'py'}, dimensions={2} | all-to-all | bytes 4194304 | tf_op jit(solution)/shard_map/while/body/eval_jaxpr/all_to_all | solution.py:72
  500.5 7.2 %reshape.145 = f32[8,1,65536]{2,1,0:T(1,128)} reshape(f32[128,2,32,64]{3,2,1,0:T(8,128)} %bitcast.327) | data formatting | bytes 4194304 | tf_op jit(solution)/shard_map/while
  511.6 48.0 %all-to-all-done.3 = f32[8,1,65536]{2,1,0:T(1,128)S(1)} async-done(((f32[8,1,65536]{2,1,0:T(1,128)}), f32[8,1,65536]{2,1,0:T(1,128)S(1)}, u32[]{:S(2)}, u32[]{:S(2)}) %all-to-all-start.3) | async-done | bytes 2097184 | tf_op jit(solution)/shard_map/while/body/eval_jaxpr/all_to_all | solution.py:71
  561.5 7.2 %reduce.5 = f32[8,65536]{1,0:T(8,128)S(1)} reduce(f32[8,1,65536]{2,1,0:T(1,128)} %copy-done, f32[]{:T(128)} %broadcast.657), dimensions={1}, to_apply=%all_to_all.189.reduce_sub_computation | reduce | bytes 4194308 | tf_op jit(solution)/shard_map/while/body/eval_jaxpr/all_to_all | solution.py:71
  572.3 7.0 %copy.154 = f32[2,16,32,8,64]{2,4,3,1,0:T(8,128)} copy(f32[2,16,32,8,64]{4,2,0,1,3:T(8,128)} %bitcast.326) | data formatting | bytes 4194304 | tf_op jit(solution)/shard_map/while/body/eval_jaxpr/all_to_all | solution.py:71
  579.3 7.9 %copy.155 = f32[2,16,32,4,8,16]{2,5,4,3,1,0:T(8,128)} copy(f32[2,16,32,4,8,16]{2,5,3,4,1,0:T(8,128)} %bitcast.320) | data formatting | bytes 4194304 | tf_op jit(solution)/shard_map/while/body/eval_jaxpr/transpose | solution.py:79
  609.6 37.5 %all-reduce = (f32[8]{0:T(128)S(1)}, f32[8]{0:T(128)S(1)}) all-reduce(f32[8]{0:T(128)S(1)} %get-tuple-element.349, f32[8]{0:T(128)S(1)} %get-tuple-element.348), channel_id=1, replica_groups=mesh['py'=4,'pz'=8] {'py','pz'}, use_global_device_ids=true, to_apply=%region_3.4 | all-reduce | flops 16 | bytes 128 | tf_op jit(solution)/shard_map/psum | solution.py:102
  651.4 41.5 %psum.23 = f32[8]{0:T(128)S(1)} all-reduce(f32[8]{0:T(128)S(1)} %multiply_reduce_fusion), channel_id=1, replica_groups=mesh['py'=4,'pz'=8] {'py','pz'}, use_global_device_ids=true, to_apply=%region_7.8 | all-reduce | flops 8 | bytes 64 | tf_op jit(solution)/shard_map/psum | solution.py:105
  (130 shorter events, 209.5 us)
Async XLA Ops:
  3.2 599.9 %copy-start.4 = (f32[16,32,128]{2,1,0:T(8,128)S(1)}, f32[16,32,128]{2,1,0:T(8,128)}, u32[]{:S(2)}) copy-start(f32[16,32,128]{2,1,0:T(8,128)} %param.7) | copy-start | bytes 786436
  81.3 54.2 %all-to-all-start.1 = ((f32[2,16,128,128]{2,1,0,3:T(8,128)}), f32[2,16,128,128]{2,1,0,3:T(8,128)S(1)}, u32[]{:S(2)}, u32[]{:S(2)}) async-start(f32[2,16,128,128]{2,1,0,3:T(8,128)} %copy.145), calls=%async_computation.1 | async-start | bytes 4194304 | tf_op jit(solution)/shard_map/while/body/eval_jaxpr/all_to_all | solution.py:54
  138.5 3.5 copy-start.1
  211.0 51.9 %all-to-all-start.3 = ((f32[8,1,65536]{2,1,0:T(1,128)}), f32[8,1,65536]{2,1,0:T(1,128)S(1)}, u32[]{:S(2)}, u32[]{:S(2)}) async-start(f32[8,1,65536]{2,1,0:T(1,128)} %reshape.145), calls=%async_computation.3 | async-start | bytes 4194304 | tf_op jit(solution)/shard_map/while/body/eval_jaxpr/all_to_all | solution.py:71
  262.9 1.4 copy-start
  298.6 2.5 copy-start.2
  301.3 2.0 copy-start.3
  380.5 51.7 %all-to-all-start.1 = ((f32[2,16,128,128]{2,1,0,3:T(8,128)}), f32[2,16,128,128]{2,1,0,3:T(8,128)S(1)}, u32[]{:S(2)}, u32[]{:S(2)}) async-start(f32[2,16,128,128]{2,1,0,3:T(8,128)} %copy.145), calls=%async_computation.1 | async-start | bytes 4194304 | tf_op jit(solution)/shard_map/while/body/eval_jaxpr/all_to_all | solution.py:54
  435.2 3.5 copy-start.1
  507.7 51.9 %all-to-all-start.3 = ((f32[8,1,65536]{2,1,0:T(1,128)}), f32[8,1,65536]{2,1,0:T(1,128)S(1)}, u32[]{:S(2)}, u32[]{:S(2)}) async-start(f32[8,1,65536]{2,1,0:T(1,128)} %reshape.145), calls=%async_computation.3 | async-start | bytes 4194304 | tf_op jit(solution)/shard_map/while/body/eval_jaxpr/all_to_all | solution.py:71
  559.6 1.4 copy-start
  595.2 2.5 copy-start.2
  598.0 2.0 copy-start.3
  647.1 4.2 copy-start.5
  647.2 45.7 %copy-start.6 = (s32[8]{0:T(128)S(1)}, s32[8]{0:T(128)}, u32[]{:S(2)}) copy-start(s32[8]{0:T(128)} %param.9) | copy-start | bytes 100
where the time goes:
time: 697 us; the launch traced here: 694 us
  blocking collectives  195 us (28%)
  waiting for transfers between devices  189 us (27%)
  local copies, waits for them, and re-layouts  156 us (22%)
  matrix products  85.4 us (12%)
  other arithmetic  44.8 us (6%)
  starting transfers between devices  18.7 us (3%)
    all_to_all x2, waiting for transfers between devices, slab_kinetic(): lax.all_to_all(lax.all_to_all(spatial, 'py', split_axis=2, concat_axis=3,...  96 us
    all_to_all x2, waiting for transfers between devices, slab_kinetic(): lax.all_to_all(lax.all_to_all(flat, 'py', split_axis=3, concat_axis=2, ti...  92.9 us
    all_to_all x2, blocking collectives, slab_kinetic(): lax.all_to_all(flat, 'py', split_axis=3, concat_axis=2, tiled=True)  59.3 us
    all_to_all x2, blocking collectives, slab_kinetic(): lax.all_to_all(spatial, 'py', split_axis=2, concat_axis=3, tiled=True)  56.3 us
    while x24, local copies, waits for them, and re-layouts  52.9 us
    psum x1, blocking collectives, body(): lax.psum(jnp.sum(residual * residual, axis=(0, 2, 3, 4)), ('py', 'pz'))  41.5 us
    psum x1, blocking collectives, body(): lax.psum((norm_local, correlation_local), ('py', 'pz'))  37.5 us
    dot_general x12, matrix products, transform_axis(): jnp.einsum(form, imag_part, sines, precision=high)  22.5 us
  transfers between devices with their start and end apart: 4, of which 4 were waited for; matrix products, arithmetic and copies ran while one was open for 0% of the time, Pallas kernels for 0%

commit v1 on v0

v1 whole, which is shorter than its diff:
```python
import functools
import math

import jax
import jax.numpy as jnp
import ml_dtypes
import numpy as np
from jax import lax
from jax.experimental import pallas as pl
from jax.experimental.pallas import tpu as pltpu
from jax.sharding import PartitionSpec as P

F32 = jnp.float32
BF16 = jnp.bfloat16


def split_table(length, inverse):
    counter = np.arange(length)
    angle = 2.0 * np.pi / length * (counter[:, None] * counter[None, :] % length)
    scale = 1.0 / length if inverse else 1.0
    sign = 1.0 if inverse else -1.0
    cosines, sines = scale * np.cos(angle), sign * scale * np.sin(angle)
    table = np.block([[cosines, -sines], [sines, cosines]]).astype(np.float32)
    high = table.astype(ml_dtypes.bfloat16)
    low = (table - high.astype(np.float32)).astype(ml_dtypes.bfloat16)
    return high, low


def split(value):
    high = value.astype(BF16)
    return high, (value - high.astype(F32)).astype(BF16)


def dot(left, right):
    return jnp.dot(left, right, preferred_element_type=F32)


def left_apply(high, low, value):
    vh, vl = split(value)
    return dot(high, vh) + (dot(high, vl) + dot(low, vh))


def right_apply(value, high, low):
    vh, vl = split(value)
    return dot(vh, high) + (dot(vl, high) + dot(vh, low))


def forward_kernel(lh, ll, rh, rl, src, dst):
    pieces, _, depth, rows, n = src.shape
    owners, width = dst.shape[0], dst.shape[3]
    planes = []
    for z in range(depth):
        part = [
            jnp.concatenate([src[s, p, z] for s in range(pieces)], axis=0) for p in range(2)
        ]
        planes.append(jnp.concatenate(part, axis=1))
    along_x = right_apply(jnp.concatenate(planes, axis=0), rh[...], rl[...])
    columns = jnp.concatenate(
        [
            jnp.concatenate(
                [along_x[z * n : (z + 1) * n, :n], along_x[z * n : (z + 1) * n, n:]], axis=0
            )
            for z in range(depth)
        ],
        axis=1,
    )
    out = left_apply(lh[...], ll[...], columns)
    for z in range(depth):
        for q in range(2):
            for d in range(owners):
                first = q * n + d * width
                dst[d, q, z] = out[first : first + width, z * n : (z + 1) * n]


def middle_kernel(scalars, fh, fl, ih, il, src, dst):
    owners, _, depth, width, n = src.shape
    planes = []
    for q in range(2):
        planes.append(jnp.swapaxes(src[:, q].reshape(owners * depth, width, n), 0, 1))
    columns = jnp.concatenate(
        [jnp.concatenate([planes[0][j], planes[1][j]], axis=0) for j in range(width)], axis=1
    )
    spectrum = left_apply(fh[...], fl[...], columns)
    kz = lax.broadcasted_iota(jnp.int32, (n, n), 0)
    kx = lax.broadcasted_iota(jnp.int32, (n, n), 1)
    kz = jnp.where(kz < n // 2, kz, kz - n)
    kx = jnp.where(kx < n // 2, kx, kx - n)
    base = kz * kz + kx * kx
    cutoff = scalars[0]
    start = scalars[1] + pl.program_id(0) * width
    kinetic = []
    for j in range(width):
        ky = start + j
        ky = jnp.where(ky < n // 2, ky, ky - n)
        total = base + ky * ky
        value = (0.5 * (math.pi / n) ** 2) * total.astype(F32)
        kinetic.append(jnp.where(total <= cutoff, value, 0.0))
    kinetic = jnp.concatenate(kinetic, axis=1)
    kinetic = jnp.concatenate([kinetic, kinetic], axis=0)
    back = left_apply(ih[...], il[...], spectrum * kinetic)
    for q in range(2):
        stacked = jnp.stack(
            [back[q * n : (q + 1) * n, j * n : (j + 1) * n] for j in range(width)], axis=0
        )
        dst[:, q] = jnp.swapaxes(stacked, 0, 1).reshape(owners, depth, width, n)


def whole(shape):
    return pl.BlockSpec(shape, lambda i: (0,) * len(shape))


PARAMS = dict(dimension_semantics=("arbitrary",), vmem_limit_bytes=40 * 1024 * 1024)


def planes_call(left, right, src, out_shape):
    depth = math.gcd(src.shape[2], 4)
    n = src.shape[4]

    def spec(shape):
        return pl.BlockSpec((shape[0], 2, depth, shape[3], n), lambda i: (0, 0, i, 0, 0))

    table = whole((2 * n, 2 * n))
    return pl.pallas_call(
        forward_kernel,
        grid=(src.shape[2] // depth,),
        in_specs=[table] * 4 + [spec(src.shape)],
        out_specs=spec(out_shape),
        out_shape=jax.ShapeDtypeStruct(out_shape, F32),
        compiler_params=pltpu.CompilerParams(**PARAMS),
    )(*left, *right, src)


def middle_call(scalars, forward, inverse, src):
    owners, _, depth, rows, n = src.shape
    width = min(8, rows)
    block = pl.BlockSpec((owners, 2, depth, width, n), lambda i: (0, 0, 0, i, 0))
    table = whole((2 * n, 2 * n))
    return pl.pallas_call(
        middle_kernel,
        grid=(rows // width,),
        in_specs=[pl.BlockSpec(memory_space=pltpu.SMEM)] + [table] * 4 + [block],
        out_specs=block,
        out_shape=jax.ShapeDtypeStruct(src.shape, F32),
        compiler_params=pltpu.CompilerParams(**PARAMS),
    )(scalars, *forward, *inverse, src)


def finish_kernel(kin, wave, pot, out, stats):
    parts = []
    norm = corr = 0.0
    for p in range(2):
        w = wave[p, 0]
        a = kin[0, p] + pot[...] * w
        out[p, 0] = a
        norm = norm + jnp.sum(jnp.sum(w * w, axis=0), keepdims=True)
        corr = corr + jnp.sum(jnp.sum(w * a, axis=0), keepdims=True)
    ratio = jnp.where(norm > 0.0, corr / jnp.where(norm > 0.0, norm, 1.0), 0.0)
    rest = 0.0
    for p in range(2):
        gap = out[p, 0] - ratio[None] * wave[p, 0]
        rest = rest + jnp.sum(jnp.sum(gap * gap, axis=0), keepdims=True)
    row = lax.broadcasted_iota(jnp.int32, stats.shape[1:], 0)
    stats[0] = jnp.where(row == 0, norm, jnp.where(row == 1, corr, rest))


def finish_call(kin, wave, pot):
    _, bands, depth, rows, n = wave.shape
    band = pl.BlockSpec((2, 1, depth, rows, n), lambda i: (0, i, 0, 0, 0))
    return pl.pallas_call(
        finish_kernel,
        grid=(bands,),
        in_specs=[
            pl.BlockSpec((1, 2, depth, rows, n), lambda i: (i, 0, 0, 0, 0)),
            band,
            whole(pot.shape),
        ],
        out_specs=[band, pl.BlockSpec((1, 8, 128), lambda i: (i, 0, 0))],
        out_shape=[
            jax.ShapeDtypeStruct(wave.shape, F32),
            jax.ShapeDtypeStruct((bands, 8, 128), F32),
        ],
        compiler_params=pltpu.CompilerParams(**PARAMS),
    )(kin, wave, pot)


def exchange(value, axis):
    return lax.all_to_all(value, axis, split_axis=0, concat_axis=0, tiled=True)


def body(wavefunctions, potential, cutoff_sq, locked_mask):
    _, bands, rows_z, rows_y, n = wavefunctions.shape
    size_y, size_z = lax.axis_size("py"), lax.axis_size("pz")
    fh, fl = split_table(n, False)
    ih, il = split_table(n, True)
    fwd, inv = (fh, fl), (ih, il)
    fwd_t = (np.ascontiguousarray(fh.T), np.ascontiguousarray(fl.T))
    inv_t = (np.ascontiguousarray(ih.T), np.ascontiguousarray(il.T))
    share = n // size_z
    scalars = jnp.stack([cutoff_sq[0], (lax.axis_index("pz") * share).astype(jnp.int32)])
    pieces = []
    for first in range(0, bands, size_y):
        pieces.append(jnp.swapaxes(wavefunctions[:, first : first + size_y], 0, 1))
    pieces = [exchange(piece, "py") for piece in pieces]
    pieces = [planes_call(fwd, fwd_t, x, (size_z, 2, rows_z, share, n)) for x in pieces]
    pieces = [exchange(piece, "pz") for piece in pieces]
    pieces = [middle_call(scalars, fwd, inv, x) for x in pieces]
    pieces = [exchange(piece, "pz") for piece in pieces]
    pieces = [planes_call(inv, inv_t, x, (size_y, 2, rows_z, rows_y, n)) for x in pieces]
    pieces = [exchange(piece, "py") for piece in pieces]
    kinetic_part = jnp.concatenate(pieces, axis=0)
    applied, stats = finish_call(kinetic_part, wavefunctions, potential)
    local = stats[:, :3, 0].T
    every = lax.all_gather(local.reshape(1, 3 * bands), ("py", "pz"), axis=0, tiled=True)
    norm, corr, rest = jnp.split(every, 3, axis=1)
    norm_sq = jnp.sum(norm, axis=0)
    rayleigh = jnp.sum(corr, axis=0) / norm_sq
    ratio = jnp.where(norm > 0.0, corr / jnp.where(norm > 0.0, norm, 1.0), 0.0)
    shift = ratio - rayleigh[None]
    residual_sq = jnp.sum(rest + shift * shift * norm, axis=0)
    residual_norm = jnp.sqrt(residual_sq / norm_sq) * (1.0 - locked_mask.astype(F32))
    return (applied, rayleigh, residual_norm)


def solution(mesh):
    in_specs = (P(None, None, "pz", "py", None), P("pz", "py", None), P(), P())
    out_specs = (P(None, None, "pz", "py", None), P(), P())
    return jax.shard_map(body, mesh=mesh, in_specs=in_specs, out_specs=out_specs, check_vma=False)
```

time: 697 us -> 416 us (0.60)
  local copies, waits for them, and re-layouts: 156 us -> 25 us
  blocking collectives: 195 us -> 94.3 us
  matrix products: 85.4 us -> 0 us
  other arithmetic: 44.8 us -> 3.02 us
  waiting for transfers between devices: 189 us -> 229 us
  Pallas kernels: 0 us -> 31.2 us
  starting transfers between devices: 18.7 us -> 30.7 us
    all_to_all x4 -> x1, blocking collectives: 116 us -> 29.2 us  [exchange(): return lax.all_to_all(value, axis, split_axis=0, concat_axis=0, tiled=True)]
    dot_general x48 -> x0, matrix products: 85.4 us -> none  [the longest x12 22.5 us: transform_axis(): jnp.einsum(form, imag_part, sines, precision=high)]
    psum x2 -> x0, blocking collectives: 79 us -> none  [the longest x1 41.5 us: body(): lax.psum(jnp.sum(residual * residual, axis=(0, 2, 3, 4)), ('py', 'pz'))]
    all_gather x0 -> x1, blocking collectives: none -> 65 us  [body(): lax.all_gather(local.reshape(1, 3 * bands), ('py', 'pz'), axis=0, tiled=T...]
    while x24 -> x0, local copies, waits for them, and re-layouts: 52.9 us -> none
    all_to_all x18 -> x0, local copies, waits for them, and re-layouts: 47.8 us -> none  [the longest x8 20.9 us: slab_kinetic(): lax.all_to_all(flat, 'py', split_axis=3, concat_axis=2, tiled=True)]
    all_to_all x4 -> x7, waiting for transfers between devices: 189 us -> 229 us  [exchange(): return lax.all_to_all(value, axis, split_axis=0, concat_axis=0, tiled=True)]
    pallas_call x0 -> x7, Pallas kernels: none -> 31.2 us  [the longest x4 17.4 us: planes_call(): pl.pallas_call(forward_kernel, grid=(src.shape[2] // depth,), in_specs=[t...]
  transfers between devices with their start and end apart: 4 -> 7, of which waited for: 4 -> 7; matrix products, arithmetic and copies ran while one was open for 0% -> 1% of each run, Pallas kernels for 0% -> 6%
where the time goes in v1:
time: 416 us; the launch traced here: 415 us
  waiting for transfers between devices  229 us (55%)
  blocking collectives  94.3 us (23%)
  Pallas kernels  31.2 us (8%)
  starting transfers between devices  30.7 us (7%)
  local copies, waits for them, and re-layouts  25 us (6%)
    all_to_all x7, waiting for transfers between devices, exchange(): return lax.all_to_all(value, axis, split_axis=0, concat_axis=0, tiled=True)  229 us
    all_gather x1, blocking collectives, body(): lax.all_gather(local.reshape(1, 3 * bands), ('py', 'pz'), axis=0, tiled=T...  65 us
    all_to_all x7, starting transfers between devices, exchange(): return lax.all_to_all(value, axis, split_axis=0, concat_axis=0, tiled=True)  30.7 us
    all_to_all x1, blocking collectives, exchange(): return lax.all_to_all(value, axis, split_axis=0, concat_axis=0, tiled=True)  29.2 us
    unnamed x49, local copies, waits for them, and re-layouts  20.7 us
    pallas_call x4, Pallas kernels, planes_call(): pl.pallas_call(forward_kernel, grid=(src.shape[2] // depth,), in_specs=[t...  17.4 us
  transfers between devices with their start and end apart: 7, of which 7 were waited for; matrix products, arithmetic and copies ran while one was open for 1% of the time, Pallas kernels for 6%

profile of v1, /device:TPU:0, one launch (start us, length us, event | category | flops | bytes accessed | tf_op | source)
XLA Modules:
  0.0 414.6 jit_solution(1763869698952125406)
XLA Ops:
  0.6 4.2 %fusion.6 = (f32[2,4,16,32,128]{4,3,2,1,0:T(8,128)S(1)}, f32[2,4,16,32,128]{4,3,2,1,0:T(8,128)}) fusion(f32[2,8,16,32,128]{4,3,2,1,0:T(8,128)} %wave.1), kind=kLoop, calls=%fused_computation.15 | loop fusion | bytes 8388608 | tf_op jit(solution)/shard_map/slice | solution.py:202
  6.4 4.3 %all-to-all-start = ((f32[4,2,16,32,128]{4,3,2,1,0:T(8,128)}), f32[4,2,16,32,128]{4,3,2,1,0:T(8,128)S(1)}, u32[]{:S(2)}, u32[]{:S(2)}) async-start(f32[4,2,16,32,128]{4,3,2,1,0:T(8,128)} %bitcast.12), calls=%async_computation | async-start | bytes 4194304 | tf_op jit(solution)/shard_map/all_to_all | solution.py:187
  13.8 22.6 %all-to-all-done.src = f32[4,2,16,32,128]{4,3,2,1,0:T(8,128)S(1)} async-done(((f32[4,2,16,32,128]{4,3,2,1,0:T(8,128)}), f32[4,2,16,32,128]{4,3,2,1,0:T(8,128)S(1)}, u32[]{:S(2)}, u32[]{:S(2)}) %all-to-all-start) | async-done | bytes 2097184 | tf_op jit(solution)/shard_map/all_to_all | solution.py:187
  37.7 3.8 all-to-all-start.4
  43.1 4.3 %shard_map.139 = f32[8,2,16,16,128]{4,3,2,1,0:T(8,128)S(1)} custom-call(bf16[256,256]{1,0:T(8,128)(2,1)S(1)} %copy-done.15, bf16[256,256]{1,0:T(8,128)(2,1)S(1)} %copy-done.14, bf16[256,256]{1,0:T(8,128)(2,1)S(1)} %copy-done.19, bf16[256,256]{1,0:T(8,128)(2,1)S(1)} %copy-done.18, f32[4,2,16,32,128]{4,3,2,1,0:T(8,128)S(1)} %copy-done.8), custom_call_target="tpu_custom_call" | custom-call | tf_op jit(solution)/shard_map/pallas_call | solution.py:123
  48.7 18.3 %all-to-all-done.4.src = f32[4,2,16,32,128]{4,3,2,1,0:T(8,128)S(1)} async-done(((f32[4,2,16,32,128]{4,3,2,1,0:T(8,128)}), f32[4,2,16,32,128]{4,3,2,1,0:T(8,128)S(1)}, u32[]{:S(2)}, u32[]{:S(2)}) %all-to-all-start.4) | async-done | bytes 2097184 | tf_op jit(solution)/shard_map/all_to_all | solution.py:187
  68.4 6.6 %all-to-all-start.1 = ((f32[8,2,16,16,128]{4,3,2,1,0:T(8,128)}), f32[8,2,16,16,128]{4,3,2,1,0:T(8,128)S(1)}, u32[]{:S(2)}, u32[]{:S(2)}) async-start(f32[8,2,16,16,128]{4,3,2,1,0:T(8,128)} %copy-done.10), calls=%async_computation.1 | async-start | bytes 4194304 | tf_op jit(solution)/shard_map/all_to_all | solution.py:187
  76.6 4.3 %shard_map.142 = f32[8,2,16,16,128]{4,3,2,1,0:T(8,128)S(1)} custom-call(bf16[256,256]{1,0:T(8,128)(2,1)S(1)} %copy-done.15, bf16[256,256]{1,0:T(8,128)(2,1)S(1)} %copy-done.14, bf16[256,256]{1,0:T(8,128)(2,1)S(1)} %copy-done.19, bf16[256,256]{1,0:T(8,128)(2,1)S(1)} %copy-done.18, f32[4,2,16,32,128]{4,3,2,1,0:T(8,128)S(1)} %copy-done.6), custom_call_target="tpu_custom_call" | custom-call | tf_op jit(solution)/shard_map/pallas_call | solution.py:123
  82.2 40.7 %all-to-all-done.1.src = f32[8,2,16,16,128]{4,3,2,1,0:T(8,128)S(1)} async-done(((f32[8,2,16,16,128]{4,3,2,1,0:T(8,128)}), f32[8,2,16,16,128]{4,3,2,1,0:T(8,128)S(1)}, u32[]{:S(2)}, u32[]{:S(2)}) %all-to-all-start.1) | async-done | bytes 2097184 | tf_op jit(solution)/shard_map/all_to_all | solution.py:187
  122.9 4.4 %all-to-all-start.5 = ((f32[8,2,16,16,128]{4,3,2,1,0:T(8,128)}), f32[8,2,16,16,128]{4,3,2,1,0:T(8,128)}, u32[]{:S(2)}, u32[]{:S(2)}) async-start(f32[8,2,16,16,128]{4,3,2,1,0:T(8,128)} %copy-done.2), calls=%async_computation.5 | async-start | bytes 4194304 | tf_op jit(solution)/shard_map/all_to_all | solution.py:187
  128.0 3.3 shard_map.140
  132.6 42.5 %all-to-all-done.5.src = f32[8,2,16,16,128]{4,3,2,1,0:T(8,128)} async-done(((f32[8,2,16,16,128]{4,3,2,1,0:T(8,128)}), f32[8,2,16,16,128]{4,3,2,1,0:T(8,128)}, u32[]{:S(2)}, u32[]{:S(2)}) %all-to-all-start.5) | async-done | bytes 2097184 | tf_op jit(solution)/shard_map/all_to_all | solution.py:187
  175.1 3.6 all-to-all-start.2
  178.7 4.7 %shard_map.143 = f32[8,2,16,16,128]{4,3,2,1,0:T(8,128)} custom-call(s32[2]{0:T(128)S(1)} %pad_add_fusion.scalars, bf16[256,256]{1,0:T(8,128)(2,1)S(1)} %copy-done.15, bf16[256,256]{1,0:T(8,128)(2,1)S(1)} %copy-done.14, bf16[256,256]{1,0:T(8,128)(2,1)S(1)} %copy-done.13, bf16[256,256]{1,0:T(8,128)(2,1)S(1)} %copy-done.12, ...), custom_call_target="tpu_custom_call" | custom-call | tf_op jit(solution)/shard_map/pallas_call | solution.py:138
  183.4 43.7 %all-to-all-done.2.src = f32[8,2,16,16,128]{4,3,2,1,0:T(8,128)S(1)} async-done(((f32[8,2,16,16,128]{4,3,2,1,0:T(8,128)}), f32[8,2,16,16,128]{4,3,2,1,0:T(8,128)S(1)}, u32[]{:S(2)}, u32[]{:S(2)}) %all-to-all-start.2) | async-done | bytes 2097184 | tf_op jit(solution)/shard_map/all_to_all | solution.py:187
  228.5 3.6 all-to-all-start.6
  233.7 4.3 %shard_map.141 = f32[4,2,16,32,128]{4,3,2,1,0:T(8,128)S(1)} custom-call(bf16[256,256]{1,0:T(8,128)(2,1)S(1)} %copy-done.13, bf16[256,256]{1,0:T(8,128)(2,1)S(1)} %copy-done.12, bf16[256,256]{1,0:T(8,128)(2,1)S(1)} %copy-done.17, bf16[256,256]{1,0:T(8,128)(2,1)S(1)} %copy-done.16, f32[8,2,16,16,128]{4,3,2,1,0:T(8,128)S(1)} %copy-done.4), custom_call_target="tpu_custom_call" | custom-call | tf_op jit(solution)/shard_map/pallas_call | solution.py:123
  239.4 41.2 %all-to-all-done.6.src = f32[8,2,16,16,128]{4,3,2,1,0:T(8,128)S(1)} async-done(((f32[8,2,16,16,128]{4,3,2,1,0:T(8,128)}), f32[8,2,16,16,128]{4,3,2,1,0:T(8,128)S(1)}, u32[]{:S(2)}, u32[]{:S(2)}) %all-to-all-start.6) | async-done | bytes 2097184 | tf_op jit(solution)/shard_map/all_to_all | solution.py:187
  280.5 4.5 %all-to-all-start.3 = ((f32[4,2,16,32,128]{4,3,2,1,0:T(8,128)}), f32[4,2,16,32,128]{4,3,2,1,0:T(8,128)}, u32[]{:S(2)}, u32[]{:S(2)}) async-start(f32[4,2,16,32,128]{4,3,2,1,0:T(8,128)} %copy-done.9), calls=%async_computation.3 | async-start | bytes 4194304 | tf_op jit(solution)/shard_map/all_to_all | solution.py:187
  285.0 4.3 %shard_map.144 = f32[4,2,16,32,128]{4,3,2,1,0:T(8,128)S(1)} custom-call(bf16[256,256]{1,0:T(8,128)(2,1)S(1)} %copy-done.13, bf16[256,256]{1,0:T(8,128)(2,1)S(1)} %copy-done.12, bf16[256,256]{1,0:T(8,128)(2,1)S(1)} %copy-done.17, bf16[256,256]{1,0:T(8,128)(2,1)S(1)} %copy-done.16, f32[8,2,16,16,128]{4,3,2,1,0:T(8,128)S(1)} %all-to-all-done.6.src), custom_call_target="tpu_custom_call" | custom-call | tf_op jit(solution)/shard_map/pallas_call | solution.py:123
  290.7 20.0 %all-to-all-done.3 = f32[4,2,16,32,128]{4,3,2,1,0:T(8,128)} async-done(((f32[4,2,16,32,128]{4,3,2,1,0:T(8,128)}), f32[4,2,16,32,128]{4,3,2,1,0:T(8,128)}, u32[]{:S(2)}, u32[]{:S(2)}) %all-to-all-start.3) | async-done | bytes 2097184 | tf_op jit(solution)/shard_map/all_to_all | solution.py:187
  310.7 29.2 %all_to_all.40 = f32[4,2,16,32,128]{4,3,2,1,0:T(8,128)S(1)} all-to-all(f32[4,2,16,32,128]{4,3,2,1,0:T(8,128)} %copy-done.11), channel_id=1, replica_groups=mesh['py'=4,'pz'=8] {'py'}, dimensions={0} | all-to-all | bytes 4194304 | tf_op jit(solution)/shard_map/all_to_all | solution.py:187
  342.8 5.8 %shard_map.145 = (f32[2,8,16,32,128]{4,3,2,1,0:T(8,128)}, f32[8,8,128]{2,1,0:T(8,128)S(1)}) custom-call(f32[8,2,16,32,128]{4,3,2,1,0:T(8,128)S(1)} %pad_maximum_fusion.kin, f32[2,8,16,32,128]{4,3,2,1,0:T(8,128)S(1)} %copy-done, f32[16,32,128]{2,1,0:T(8,128)S(1)} %copy-done.20), custom_call_target="tpu_custom_call" | custom-call | tf_op jit(solution)/shard_map/pallas_call | solution.py:169
  348.9 65.0 %all-gather = f32[32,1,24]{2,1,0:T(1,128)S(1)} all-gather(f32[1,1,24]{2,1,0:T(1,128)S(1)} %reshape.15), channel_id=1, replica_groups=mesh['py'=4,'pz'=8] {'py','pz'}, dimensions={0}, use_global_device_ids=true | all-gather | bytes 3168 | tf_op jit(solution)/shard_map/all_gather | solution.py:213
  (57 shorter events, 23.8 us)
Async XLA Ops:
  6.4 29.9 %all-to-all-start = ((f32[4,2,16,32,128]{4,3,2,1,0:T(8,128)}), f32[4,2,16,32,128]{4,3,2,1,0:T(8,128)S(1)}, u32[]{:S(2)}, u32[]{:S(2)}) async-start(f32[4,2,16,32,128]{4,3,2,1,0:T(8,128)} %bitcast.12), calls=%async_computation | async-start | bytes 4194304 | tf_op jit(solution)/shard_map/all_to_all | solution.py:187
  37.7 3.8 copy-start.14
  37.7 3.8 copy-start.15
  37.7 3.8 copy-start.18
  37.7 3.8 copy-start.19
  37.7 29.4 %all-to-all-start.4 = ((f32[4,2,16,32,128]{4,3,2,1,0:T(8,128)}), f32[4,2,16,32,128]{4,3,2,1,0:T(8,128)S(1)}, u32[]{:S(2)}, u32[]{:S(2)}) async-start(f32[4,2,16,32,128]{4,3,2,1,0:T(8,128)} %bitcast.11), calls=%async_computation.4 | async-start | bytes 4194304 | tf_op jit(solution)/shard_map/all_to_all | solution.py:187
  41.5 1.6 copy-start.8
  68.4 54.5 %all-to-all-start.1 = ((f32[8,2,16,16,128]{4,3,2,1,0:T(8,128)}), f32[8,2,16,16,128]{4,3,2,1,0:T(8,128)S(1)}, u32[]{:S(2)}, u32[]{:S(2)}) async-start(f32[8,2,16,16,128]{4,3,2,1,0:T(8,128)} %copy-done.10), calls=%async_computation.1 | async-start | bytes 4194304 | tf_op jit(solution)/shard_map/all_to_all | solution.py:187
  75.0 1.6 copy-start.6
  80.9 1.3 copy-start.2
  82.2 45.8 %copy-start.12 = (bf16[256,256]{1,0:T(8,128)(2,1)S(1)}, bf16[256,256]{1,0:T(8,128)(2,1)}, u32[]{:S(2)}) copy-start(bf16[256,256]{1,0:T(8,128)(2,1)} %constant.33.clone.il.ll) | copy-start | bytes 393220
  82.2 45.8 %copy-start.13 = (bf16[256,256]{1,0:T(8,128)(2,1)S(1)}, bf16[256,256]{1,0:T(8,128)(2,1)}, u32[]{:S(2)}) copy-start(bf16[256,256]{1,0:T(8,128)(2,1)} %constant.32.clone.ih.lh) | copy-start | bytes 393220
  122.9 52.2 %all-to-all-start.5 = ((f32[8,2,16,16,128]{4,3,2,1,0:T(8,128)}), f32[8,2,16,16,128]{4,3,2,1,0:T(8,128)}, u32[]{:S(2)}, u32[]{:S(2)}) async-start(f32[8,2,16,16,128]{4,3,2,1,0:T(8,128)} %copy-done.2), calls=%async_computation.5 | async-start | bytes 4194304 | tf_op jit(solution)/shard_map/all_to_all | solution.py:187
  175.1 52.0 %all-to-all-start.2 = ((f32[8,2,16,16,128]{4,3,2,1,0:T(8,128)}), f32[8,2,16,16,128]{4,3,2,1,0:T(8,128)S(1)}, u32[]{:S(2)}, u32[]{:S(2)}) async-start(f32[8,2,16,16,128]{4,3,2,1,0:T(8,128)} %copy-done.1), calls=%async_computation.2 | async-start | bytes 4194304 | tf_op jit(solution)/shard_map/all_to_all | solution.py:187
  183.4 48.7 %copy-start.16 = (bf16[256,256]{1,0:T(8,128)(2,1)S(1)}, bf16[256,256]{1,0:T(8,128)(2,1)}, u32[]{:S(2)}) copy-start(bf16[256,256]{1,0:T(8,128)(2,1)} %constant.35.clone.rl) | copy-start | bytes 393220
  183.4 48.7 %copy-start.17 = (bf16[256,256]{1,0:T(8,128)(2,1)S(1)}, bf16[256,256]{1,0:T(8,128)(2,1)}, u32[]{:S(2)}) copy-start(bf16[256,256]{1,0:T(8,128)(2,1)} %constant.34.clone.rh) | copy-start | bytes 393220
  227.1 1.3 copy-start.3
  228.5 52.1 %all-to-all-start.6 = ((f32[8,2,16,16,128]{4,3,2,1,0:T(8,128)}), f32[8,2,16,16,128]{4,3,2,1,0:T(8,128)S(1)}, u32[]{:S(2)}, u32[]{:S(2)}) async-start(f32[8,2,16,16,128]{4,3,2,1,0:T(8,128)} %shard_map.143), calls=%async_computation.6 | async-start | bytes 4194304 | tf_op jit(solution)/shard_map/all_to_all | solution.py:187
  232.1 1.6 copy-start.4
  280.5 30.2 %all-to-all-start.3 = ((f32[4,2,16,32,128]{4,3,2,1,0:T(8,128)}), f32[4,2,16,32,128]{4,3,2,1,0:T(8,128)}, u32[]{:S(2)}, u32[]{:S(2)}) async-start(f32[4,2,16,32,128]{4,3,2,1,0:T(8,128)} %copy-done.9), calls=%async_computation.3 | async-start | bytes 4194304 | tf_op jit(solution)/shard_map/all_to_all | solution.py:187
  289.4 1.3 copy-start.11
  340.0 2.8 copy-start
  340.0 2.8 copy-start.20
  342.8 71.3 %copy-start.22 = (s32[8]{0:T(128)S(1)}, s32[8]{0:T(128)}, u32[]{:S(2)}) copy-start(s32[8]{0:T(128)} %param.15) | copy-start | bytes 100
  (6 other events, 7.2 us)

commit v2 on v1

--- a/solution.py
+++ b/solution.py
@@ -1,4 +1,3 @@
-import functools
 import math
 
 import jax
@@ -45,13 +44,14 @@
     return dot(vh, high) + (dot(vl, high) + dot(vh, low))
 
 
-def forward_kernel(lh, ll, rh, rl, src, dst):
+def planes_kernel(order, lh, ll, rh, rl, src, dst):
     pieces, _, depth, rows, n = src.shape
     owners, width = dst.shape[0], dst.shape[3]
     planes = []
     for z in range(depth):
         part = [
-            jnp.concatenate([src[s, p, z] for s in range(pieces)], axis=0) for p in range(2)
+            jnp.concatenate([src[s ^ order[0], p, z] for s in range(pieces)], axis=0)
+            for p in range(2)
         ]
         planes.append(jnp.concatenate(part, axis=1))
     along_x = right_apply(jnp.concatenate(planes, axis=0), rh[...], rl[...])
@@ -69,7 +69,7 @@
         for q in range(2):
             for d in range(owners):
                 first = q * n + d * width
-                dst[d, q, z] = out[first : first + width, z * n : (z + 1) * n]
+                dst[d ^ order[1], q, z] = out[first : first + width, z * n : (z + 1) * n]
 
 
 def middle_kernel(scalars, fh, fl, ih, il, src, dst):
@@ -112,7 +112,7 @@
 PARAMS = dict(dimension_semantics=("arbitrary",), vmem_limit_bytes=40 * 1024 * 1024)
 
 
-def planes_call(left, right, src, out_shape):
+def planes_call(order, left, right, src, out_shape):
     depth = math.gcd(src.shape[2], 4)
     n = src.shape[4]
 
@@ -121,13 +121,13 @@
 
     table = whole((2 * n, 2 * n))
     return pl.pallas_call(
-        forward_kernel,
+        planes_kernel,
         grid=(src.shape[2] // depth,),
-        in_specs=[table] * 4 + [spec(src.shape)],
+        in_specs=[pl.BlockSpec(memory_space=pltpu.SMEM)] + [table] * 4 + [spec(src.shape)],
         out_specs=spec(out_shape),
         out_shape=jax.ShapeDtypeStruct(out_shape, F32),
         compiler_params=pltpu.CompilerParams(**PARAMS),
-    )(*left, *right, src)
+    )(order, *left, *right, src)
 
 
 def middle_call(scalars, forward, inverse, src):
@@ -145,8 +145,8 @@
     )(scalars, *forward, *inverse, src)
 
 
-def finish_kernel(kin, wave, pot, out, stats):
-    parts = []
+def finish_kernel(me, kin, wave, pot, *refs):
+    out, stats = refs[-2:]
     norm = corr = 0.0
     for p in range(2):
         w = wave[p, 0]
@@ -163,28 +163,63 @@
     stats[0] = jnp.where(row == 0, norm, jnp.where(row == 1, corr, rest))
 
 
-def finish_call(kin, wave, pot):
+def finish_call(me, kin, wave, pot, first, applied):
     _, bands, depth, rows, n = wave.shape
-    band = pl.BlockSpec((2, 1, depth, rows, n), lambda i: (0, i, 0, 0, 0))
+    count = kin.shape[0]
+    band = pl.BlockSpec((2, 1, depth, rows, n), lambda i, me: (0, first + (i ^ me[0]), 0, 0, 0))
+    in_specs = [
+        pl.BlockSpec((1, 2, depth, rows, n), lambda i, me: (i, 0, 0, 0, 0)),
+        band,
+        pl.BlockSpec(pot.shape, lambda i, me: (0, 0, 0)),
+    ]
+    args, aliases = [me, kin, wave, pot], {}
+    if applied is not None:
+        in_specs.append(pl.BlockSpec(memory_space=pl.ANY))
+        args.append(applied)
+        aliases = {4: 0}
     return pl.pallas_call(
         finish_kernel,
-        grid=(bands,),
-        in_specs=[
-            pl.BlockSpec((1, 2, depth, rows, n), lambda i: (i, 0, 0, 0, 0)),
-            band,
-            whole(pot.shape),
-        ],
-        out_specs=[band, pl.BlockSpec((1, 8, 128), lambda i: (i, 0, 0))],
+        grid_spec=pltpu.PrefetchScalarGridSpec(
+            num_scalar_prefetch=1,
+            grid=(count,),
+            in_specs=in_specs,
+            out_specs=[band, pl.BlockSpec((1, 8, 128), lambda i, me: (i ^ me[0], 0, 0))],
+        ),
         out_shape=[
             jax.ShapeDtypeStruct(wave.shape, F32),
-            jax.ShapeDtypeStruct((bands, 8, 128), F32),
+            jax.ShapeDtypeStruct((count, 8, 128), F32),
         ],
+        input_output_aliases=aliases,
         compiler_params=pltpu.CompilerParams(**PARAMS),
-    )(kin, wave, pot)
+    )(*args)
 
 
 def exchange(value, axis):
     return lax.all_to_all(value, axis, split_axis=0, concat_axis=0, tiled=True)
+
+
+def swap(pieces, axis):
+    size = len(pieces)
+    return jnp.stack(
+        [pieces[0]]
+        + [
+            lax.ppermute(pieces[d], axis, [(i, i ^ d) for i in range(size)])
+            for d in range(1, size)
+        ]
+    )
+
+
+def merge(stats, axis):
+    size = lax.axis_size(axis)
+    every = exchange(jnp.broadcast_to(stats[None], (size,) + stats.shape), axis)
+    norm, corr, rest = every[:, 0], every[:, 1], every[:, 2]
+    norm_all, corr_all = jnp.sum(norm, axis=0), jnp.sum(corr, axis=0)
+    gap = ratio_of(corr, norm) - ratio_of(corr_all, norm_all)[None]
+    return jnp.stack([norm_all, corr_all, jnp.sum(rest + gap * gap * norm, axis=0)])
+
+
+def ratio_of(corr, norm):
+    return jnp.where(norm > 0.0, corr / jnp.where(norm > 0.0, norm, 1.0), 0.0)
 
 
 def body(wavefunctions, potential, cutoff_sq, locked_mask):
@@ -197,27 +232,36 @@
     inv_t = (np.ascontiguousarray(ih.T), np.ascontiguousarray(il.T))
     share = n // size_z
     scalars = jnp.stack([cutoff_sq[0], (lax.axis_index("pz") * share).astype(jnp.int32)])
-    pieces = []
+    me = lax.axis_index("py").astype(jnp.int32)
+    there, back = jnp.stack([me, 0 * me]), jnp.stack([0 * me, me])
+    spectra = []
+    gathered = None
     for first in range(0, bands, size_y):
-        pieces.append(jnp.swapaxes(wavefunctions[:, first : first + size_y], 0, 1))
-    pieces = [exchange(piece, "py") for piece in pieces]
-    pieces = [planes_call(fwd, fwd_t, x, (size_z, 2, rows_z, share, n)) for x in pieces]
+        source = wavefunctions
+        if gathered is not None:
+            source, gathered = lax.optimization_barrier((source, gathered))
+            spectra[-1] = gathered
+        sent = [
+            lax.dynamic_index_in_dim(source, first + (me ^ d), 1, keepdims=False)
+            for d in range(size_y)
+        ]
+        gathered = swap(sent, "py")
+        spectra.append(gathered)
+    pieces = [planes_call(there, fwd, fwd_t, x, (size_z, 2, rows_z, share, n)) for x in spectra]
     pieces = [exchange(piece, "pz") for piece in pieces]
     pieces = [middle_call(scalars, fwd, inv, x) for x in pieces]
     pieces = [exchange(piece, "pz") for piece in pieces]
-    pieces = [planes_call(inv, inv_t, x, (size_y, 2, rows_z, rows_y, n)) for x in pieces]
-    pieces = [exchange(piece, "py") for piece in pieces]
-    kinetic_part = jnp.concatenate(pieces, axis=0)
-    applied, stats = finish_call(kinetic_part, wavefunctions, potential)
-    local = stats[:, :3, 0].T
-    every = lax.all_gather(local.reshape(1, 3 * bands), ("py", "pz"), axis=0, tiled=True)
-    norm, corr, rest = jnp.split(every, 3, axis=1)
-    norm_sq = jnp.sum(norm, axis=0)
-    rayleigh = jnp.sum(corr, axis=0) / norm_sq
-    ratio = jnp.where(norm > 0.0, corr / jnp.where(norm > 0.0, norm, 1.0), 0.0)
-    shift = ratio - rayleigh[None]
-    residual_sq = jnp.sum(rest + shift * shift * norm, axis=0)
-    residual_norm = jnp.sqrt(residual_sq / norm_sq) * (1.0 - locked_mask.astype(F32))
+    pieces = [planes_call(back, inv, inv_t, x, (size_y, 2, rows_z, rows_y, n)) for x in pieces]
+    applied, stats = None, []
+    for index, piece in enumerate(pieces):
+        kinetic_part = swap([piece[d] for d in range(size_y)], "py")
+        applied, some = finish_call(
+            me[None], kinetic_part, wavefunctions, potential, index * size_y, applied
+        )
+        stats.append(some[:, :3, 0])
+    total = merge(merge(jnp.concatenate(stats, axis=0).T, "py"), "pz")
+    rayleigh = total[1] / total[0]
+    residual_norm = jnp.sqrt(total[2] / total[0]) * (1.0 - locked_mask.astype(F32))
     return (applied, rayleigh, residual_norm)
 
 

time: 416 us -> 301 us (0.72)
  blocking collectives: 94.3 us -> 16.5 us
  waiting for transfers between devices: 229 us -> 204 us
  local copies, waits for them, and re-layouts: 25 us -> 13.7 us
    all_to_all x7 -> x4, waiting for transfers between devices: 229 us -> 140 us  [exchange(): return lax.all_to_all(value, axis, split_axis=0, concat_axis=0, tiled=True)]
    all_gather x1 -> x0, blocking collectives: 65 us -> none  [body(): lax.all_gather(local.reshape(1, 3 * bands), ('py', 'pz'), axis=0, tiled=T...]
    ppermute x0 -> x12, waiting for transfers between devices: none -> 64.3 us  [swap(): lax.ppermute(pieces[d], axis, [(i, i ^ d) for i in range(size)])]
    all_to_all x1 -> x2, blocking collectives: 29.2 us -> 16.5 us  [exchange(): return lax.all_to_all(value, axis, split_axis=0, concat_axis=0, tiled=True)]
    all_to_all x7 -> x4, starting transfers between devices: 30.7 us -> 18.2 us  [exchange(): return lax.all_to_all(value, axis, split_axis=0, concat_axis=0, tiled=True)]
    unnamed x49 -> x32, local copies, waits for them, and re-layouts: 20.7 us -> 8.71 us
    ppermute x0 -> x12, starting transfers between devices: none -> 8.89 us  [swap(): lax.ppermute(pieces[d], axis, [(i, i ^ d) for i in range(size)])]
    pallas_call x5 -> x6, Pallas kernels: 23.2 us -> 26.5 us  [the longest x4 20 us: planes_call(): pl.pallas_call(planes_kernel, grid=(src.shape[2] // depth,), in_specs=[pl...]
  transfers between devices with their start and end apart: 7 -> 16, of which waited for: 7 -> 10; matrix products, arithmetic and copies ran while one was open for 1% -> 2% of each run, Pallas kernels for 6% -> 9%
where the time goes in v2:
time: 301 us
  waiting for transfers between devices  204 us (68%)
  Pallas kernels  34.5 us (11%)
  starting transfers between devices  27.1 us (9%)
  blocking collectives  16.5 us (5%)
  local copies, waits for them, and re-layouts  13.7 us (5%)
  other arithmetic  3.71 us (1%)
    all_to_all x4, waiting for transfers between devices, exchange(): return lax.all_to_all(value, axis, split_axis=0, concat_axis=0, tiled=True)  140 us
    ppermute x12, waiting for transfers between devices, swap(): lax.ppermute(pieces[d], axis, [(i, i ^ d) for i in range(size)])  64.3 us
    pallas_call x4, Pallas kernels, planes_call(): pl.pallas_call(planes_kernel, grid=(src.shape[2] // depth,), in_specs=[pl...  20 us
    all_to_all x4, starting transfers between devices, exchange(): return lax.all_to_all(value, axis, split_axis=0, concat_axis=0, tiled=True)  18.2 us
    all_to_all x2, blocking collectives, exchange(): return lax.all_to_all(value, axis, split_axis=0, concat_axis=0, tiled=True)  16.5 us
    ppermute x12, starting transfers between devices, swap(): lax.ppermute(pieces[d], axis, [(i, i ^ d) for i in range(size)])  8.89 us
    unnamed x32, local copies, waits for them, and re-layouts  8.71 us
    pallas_call x2, Pallas kernels, middle_call(): pl.pallas_call(middle_kernel, grid=(rows // width,), in_specs=[pl.BlockSp...  7.99 us
  transfers between devices with their start and end apart: 16, of which 10 were waited for; matrix products, arithmetic and copies ran while one was open for 2% of the time, Pallas kernels for 9%

profile of v2, /device:TPU:0, one launch (start us, length us, event | category | flops | bytes accessed | tf_op | source)
XLA Modules:
  0.0 300.9 jit_solution(13368934490265106615)
XLA Ops:
  5.6 11.6 %collective-permute-done.2 = f32[2,16,32,128]{3,2,1,0:T(8,128)S(1)} collective-permute-done((f32[2,16,32,128]{3,2,1,0:T(8,128)S(1)}, f32[2,16,32,128]{3,2,1,0:T(8,128)S(1)}, u32[]{:S(2)}, u32[]{:S(2)}) %collective-permute-start.2) | collective-permute-done | bytes 524320 | tf_op jit(solution)/shard_map/ppermute | solution.py:206
  17.2 11.4 %collective-permute-done.1 = f32[2,16,32,128]{3,2,1,0:T(8,128)S(1)} collective-permute-done((f32[2,16,32,128]{3,2,1,0:T(8,128)S(1)}, f32[2,16,32,128]{3,2,1,0:T(8,128)S(1)}, u32[]{:S(2)}, u32[]{:S(2)}) %collective-permute-start.1) | collective-permute-done | bytes 524320 | tf_op jit(solution)/shard_map/ppermute | solution.py:206
  29.7 5.0 %shard_map.142 = f32[8,2,16,16,128]{4,3,2,1,0:T(8,128)S(1)} custom-call(s32[2]{0:T(128)S(1)} %pad_add_fusion.2.order, bf16[256,256]{1,0:T(8,128)(2,1)S(1)} %copy-done.9, bf16[256,256]{1,0:T(8,128)(2,1)S(1)} %copy-done.8, bf16[256,256]{1,0:T(8,128)(2,1)S(1)} %copy-done.14, bf16[256,256]{1,0:T(8,128)(2,1)S(1)} %copy-done.13, ...), custom_call_target="tpu_custom_call" | custom-call | tf_op jit(solution)/shard_map/pallas_call | solution.py:123
  36.0 6.6 %all-to-all-start.2 = ((f32[8,2,16,16,128]{4,3,2,1,0:T(8,128)}), f32[8,2,16,16,128]{4,3,2,1,0:T(8,128)S(1)}, u32[]{:S(2)}, u32[]{:S(2)}) async-start(f32[8,2,16,16,128]{4,3,2,1,0:T(8,128)} %copy-done.1), calls=%async_computation.2 | async-start | bytes 4194304 | tf_op jit(solution)/shard_map/all_to_all | solution.py:198
  46.2 12.3 %collective-permute-done.5 = f32[2,16,32,128]{3,2,1,0:T(8,128)S(1)} collective-permute-done((f32[2,16,32,128]{3,2,1,0:T(8,128)S(1)}, f32[2,16,32,128]{3,2,1,0:T(8,128)S(1)}, u32[]{:S(2)}, u32[]{:S(2)}) %collective-permute-start.5) | collective-permute-done | bytes 524320 | tf_op jit(solution)/shard_map/ppermute | solution.py:206
  58.5 11.3 %collective-permute-done.4 = f32[2,16,32,128]{3,2,1,0:T(8,128)S(1)} collective-permute-done((f32[2,16,32,128]{3,2,1,0:T(8,128)S(1)}, f32[2,16,32,128]{3,2,1,0:T(8,128)S(1)}, u32[]{:S(2)}, u32[]{:S(2)}) %collective-permute-start.4) | collective-permute-done | bytes 524320 | tf_op jit(solution)/shard_map/ppermute | solution.py:206
  70.0 5.0 %shard_map.139 = f32[8,2,16,16,128]{4,3,2,1,0:T(8,128)S(1)} custom-call(s32[2]{0:T(128)S(1)} %pad_add_fusion.2.order, bf16[256,256]{1,0:T(8,128)(2,1)S(1)} %copy-done.9, bf16[256,256]{1,0:T(8,128)(2,1)S(1)} %copy-done.8, bf16[256,256]{1,0:T(8,128)(2,1)S(1)} %copy-done.14, bf16[256,256]{1,0:T(8,128)(2,1)S(1)} %copy-done.13, ...), custom_call_target="tpu_custom_call" | custom-call | tf_op jit(solution)/shard_map/pallas_call | solution.py:123
  76.4 14.7 %all-to-all-done.2.src = f32[8,2,16,16,128]{4,3,2,1,0:T(8,128)S(1)} async-done(((f32[8,2,16,16,128]{4,3,2,1,0:T(8,128)}), f32[8,2,16,16,128]{4,3,2,1,0:T(8,128)S(1)}, u32[]{:S(2)}, u32[]{:S(2)}) %all-to-all-start.2) | async-done | bytes 2097184 | tf_op jit(solution)/shard_map/all_to_all | solution.py:198
  91.0 4.3 %all-to-all-start = ((f32[8,2,16,16,128]{4,3,2,1,0:T(8,128)}), f32[8,2,16,16,128]{4,3,2,1,0:T(8,128)}, u32[]{:S(2)}, u32[]{:S(2)}) async-start(f32[8,2,16,16,128]{4,3,2,1,0:T(8,128)} %copy-done.2), calls=%async_computation | async-start | bytes 4194304 | tf_op jit(solution)/shard_map/all_to_all | solution.py:198
  96.1 3.3 %shard_map.143 = f32[8,2,16,16,128]{4,3,2,1,0:T(8,128)S(1)} custom-call(s32[2]{0:T(128)S(1)} %pad_add_fusion.1.scalars, bf16[256,256]{1,0:T(8,128)(2,1)S(1)} %copy-done.9, bf16[256,256]{1,0:T(8,128)(2,1)S(1)} %copy-done.8, bf16[256,256]{1,0:T(8,128)(2,1)S(1)} %copy-done.7, bf16[256,256]{1,0:T(8,128)(2,1)S(1)} %copy-done.6, ...), custom_call_target="tpu_custom_call" | custom-call | tf_op jit(solution)/shard_map/pallas_call | solution.py:138
  100.7 42.5 %all-to-all-done.src = f32[8,2,16,16,128]{4,3,2,1,0:T(8,128)} async-done(((f32[8,2,16,16,128]{4,3,2,1,0:T(8,128)}), f32[8,2,16,16,128]{4,3,2,1,0:T(8,128)}, u32[]{:S(2)}, u32[]{:S(2)}) %all-to-all-start) | async-done | bytes 2097184 | tf_op jit(solution)/shard_map/all_to_all | solution.py:198
  143.2 3.6 %all-to-all-start.3 = ((f32[8,2,16,16,128]{4,3,2,1,0:T(8,128)}), f32[8,2,16,16,128]{4,3,2,1,0:T(8,128)S(1)}, u32[]{:S(2)}, u32[]{:S(2)}) async-start(f32[8,2,16,16,128]{4,3,2,1,0:T(8,128)} %copy-done.5), calls=%async_computation.3 | async-start | bytes 4194304 | tf_op jit(solution)/shard_map/all_to_all | solution.py:198
  146.9 4.7 %shard_map.140 = f32[8,2,16,16,128]{4,3,2,1,0:T(8,128)} custom-call(s32[2]{0:T(128)S(1)} %pad_add_fusion.1.scalars, bf16[256,256]{1,0:T(8,128)(2,1)S(1)} %copy-done.9, bf16[256,256]{1,0:T(8,128)(2,1)S(1)} %copy-done.8, bf16[256,256]{1,0:T(8,128)(2,1)S(1)} %copy-done.7, bf16[256,256]{1,0:T(8,128)(2,1)S(1)} %copy-done.6, f32[8,2,16,16,128]{4,3,2,1,0:T(8,128)} %all-to-all-done.src), custom_call_target="tpu_custom_call" | custom-call | tf_op jit(solution)/shard_map/pallas_call | solution.py:138
  151.6 43.7 %all-to-all-done.3.src = f32[8,2,16,16,128]{4,3,2,1,0:T(8,128)S(1)} async-done(((f32[8,2,16,16,128]{4,3,2,1,0:T(8,128)}), f32[8,2,16,16,128]{4,3,2,1,0:T(8,128)S(1)}, u32[]{:S(2)}, u32[]{:S(2)}) %all-to-all-start.3) | async-done | bytes 2097184 | tf_op jit(solution)/shard_map/all_to_all | solution.py:198
  196.6 3.6 %all-to-all-start.1 = ((f32[8,2,16,16,128]{4,3,2,1,0:T(8,128)}), f32[8,2,16,16,128]{4,3,2,1,0:T(8,128)S(1)}, u32[]{:S(2)}, u32[]{:S(2)}) async-start(f32[8,2,16,16,128]{4,3,2,1,0:T(8,128)} %shard_map.140), calls=%async_computation.1 | async-start | bytes 4194304 | tf_op jit(solution)/shard_map/all_to_all | solution.py:198
  201.9 5.0 %shard_map.144 = f32[4,2,16,32,128]{4,3,2,1,0:T(8,128)S(1)} custom-call(s32[2]{0:T(128)S(1)} %pad_add_fusion.order, bf16[256,256]{1,0:T(8,128)(2,1)S(1)} %copy-done.7, bf16[256,256]{1,0:T(8,128)(2,1)S(1)} %copy-done.6, bf16[256,256]{1,0:T(8,128)(2,1)S(1)} %copy-done.12, bf16[256,256]{1,0:T(8,128)(2,1)S(1)} %copy-done.11, f32[8,2,16,16,128]{4,3,2,1,0:T(8,128)S(1)} %copy-done.4), custom_call_target="tpu_custom_call" | custom-call | tf_op jit(solution)/shard_map/pallas_call | solution.py:123
  210.0 38.7 %all-to-all-done.1.src = f32[8,2,16,16,128]{4,3,2,1,0:T(8,128)S(1)} async-done(((f32[8,2,16,16,128]{4,3,2,1,0:T(8,128)}), f32[8,2,16,16,128]{4,3,2,1,0:T(8,128)S(1)}, u32[]{:S(2)}, u32[]{:S(2)}) %all-to-all-start.1) | async-done | bytes 2097184 | tf_op jit(solution)/shard_map/all_to_all | solution.py:198
  248.7 5.0 %shard_map.141 = f32[4,2,16,32,128]{4,3,2,1,0:T(8,128)S(1)} custom-call(s32[2]{0:T(128)S(1)} %pad_add_fusion.order, bf16[256,256]{1,0:T(8,128)(2,1)S(1)} %copy-done.7, bf16[256,256]{1,0:T(8,128)(2,1)S(1)} %copy-done.6, bf16[256,256]{1,0:T(8,128)(2,1)S(1)} %copy-done.12, bf16[256,256]{1,0:T(8,128)(2,1)S(1)} %copy-done.11, ...), custom_call_target="tpu_custom_call" | custom-call | tf_op jit(solution)/shard_map/pallas_call | solution.py:123
  258.5 3.2 %shard_map.145 = (f32[2,8,16,32,128]{4,3,2,1,0:T(8,128)}, f32[4,8,128]{2,1,0:T(8,128)S(1)}) custom-call(s32[1]{0:T(128)} %bitcast.me, f32[4,2,16,32,128]{4,3,2,1,0:T(8,128)S(1)} %pad_maximum_fusion.3.kin, f32[2,8,16,32,128]{4,3,2,1,0:T(8,128)S(1)} %copy-done, f32[16,32,128]{2,1,0:T(8,128)S(1)} %copy-done.10), custom_call_target="tpu_custom_call" | custom-call | tf_op jit(solution)/shard_map/pallas_call | solution.py:180
  261.8 6.3 %collective-permute-done.8 = f32[2,16,32,128]{3,2,1,0:T(8,128)S(1)} collective-permute-done((f32[2,16,32,128]{3,2,1,0:T(8,128)S(1)}, f32[2,16,32,128]{3,2,1,0:T(8,128)S(1)}, u32[]{:S(2)}, u32[]{:S(2)}) %collective-permute-start.8) | collective-permute-done | bytes 524320 | tf_op jit(solution)/shard_map/ppermute | solution.py:206
  268.1 11.4 %collective-permute-done.7 = f32[2,16,32,128]{3,2,1,0:T(8,128)S(1)} collective-permute-done((f32[2,16,32,128]{3,2,1,0:T(8,128)S(1)}, f32[2,16,32,128]{3,2,1,0:T(8,128)S(1)}, u32[]{:S(2)}, u32[]{:S(2)}) %collective-permute-start.7) | collective-permute-done | bytes 524320 | tf_op jit(solution)/shard_map/ppermute | solution.py:206
  279.7 3.3 %shard_map.146 = (f32[2,8,16,32,128]{4,3,2,1,0:T(8,128)}, f32[4,8,128]{2,1,0:T(8,128)S(1)}) custom-call(s32[1]{0:T(128)} %bitcast.me, f32[4,2,16,32,128]{4,3,2,1,0:T(8,128)S(1)} %pad_maximum_fusion.2.kin, f32[2,8,16,32,128]{4,3,2,1,0:T(8,128)S(1)} %copy-done, f32[16,32,128]{2,1,0:T(8,128)S(1)} %copy-done.10, ...), custom_call_target="tpu_custom_call", output_to_operand_aliasing={{0}: (4, {})} | custom-call | tf_op jit(solution)/shard_map/pallas_call | solution.py:180
  283.2 6.1 %all_to_all.30 = f32[4,3,8]{2,1,0:T(4,128)S(1)} all-to-all(f32[4,3,8]{2,1,0:T(4,128)S(1)} %broadcast_in_dim.36), channel_id=1, replica_groups=mesh['py'=4,'pz'=8] {'py'}, dimensions={0} | all-to-all | bytes 768 | tf_op jit(solution)/shard_map/all_to_all | solution.py:198
  289.4 10.3 %all_to_all.31 = f32[8,3,8]{2,1,0:T(4,128)S(1)} all-to-all(f32[8,3,8]{2,1,0:T(4,128)S(1)} %broadcast_in_dim.39), channel_id=1, replica_groups=mesh['py'=4,'pz'=8] {'pz'}, dimensions={0} | all-to-all | bytes 1536 | tf_op jit(solution)/shard_map/all_to_all | solution.py:198
  (76 shorter events, 26.4 us)
Async XLA Ops:
  2.4 14.8 %collective-permute-start.2 = (f32[2,16,32,128]{3,2,1,0:T(8,128)S(1)}, f32[2,16,32,128]{3,2,1,0:T(8,128)S(1)}, u32[]{:S(2)}, u32[]{:S(2)}) collective-permute-start(f32[2,16,32,128]{3,2,1,0:T(8,128)S(1)} %get-tuple-element.22), channel_id=1, source_target_pairs={{0,24},{8,16},{16,8},{24,0},{1,25},{9,17},{17,9},{25,1},{2,26},{10... | collective-permute-start | bytes 1572872 | tf_op jit(solution)/shard_map/ppermute | solution.py:206
  4.9 23.7 %collective-permute-start.1 = (f32[2,16,32,128]{3,2,1,0:T(8,128)S(1)}, f32[2,16,32,128]{3,2,1,0:T(8,128)S(1)}, u32[]{:S(2)}, u32[]{:S(2)}) collective-permute-start(f32[2,16,32,128]{3,2,1,0:T(8,128)S(1)} %get-tuple-element.23), channel_id=1, source_target_pairs={{0,16},{8,24},{16,0},{24,8},{1,17},{9,25},{17,1},{25,9},{2,18},{10... | collective-permute-start | bytes 1572872 | tf_op jit(solution)/shard_map/ppermute | solution.py:206
  5.5 23.1 %collective-permute-start = (f32[2,16,32,128]{3,2,1,0:T(8,128)S(1)}, f32[2,16,32,128]{3,2,1,0:T(8,128)S(1)}, u32[]{:S(2)}, u32[]{:S(2)}) collective-permute-start(f32[2,16,32,128]{3,2,1,0:T(8,128)S(1)} %get-tuple-element.24), channel_id=1, source_target_pairs={{0,8},{8,0},{16,24},{24,16},{1,9},{9,1},{17,25},{25,17},{2,10},{10... | collective-permute-start | bytes 1572872 | tf_op jit(solution)/shard_map/ppermute | solution.py:206
  36.0 55.0 %all-to-all-start.2 = ((f32[8,2,16,16,128]{4,3,2,1,0:T(8,128)}), f32[8,2,16,16,128]{4,3,2,1,0:T(8,128)S(1)}, u32[]{:S(2)}, u32[]{:S(2)}) async-start(f32[8,2,16,16,128]{4,3,2,1,0:T(8,128)} %copy-done.1), calls=%async_computation.2 | async-start | bytes 4194304 | tf_op jit(solution)/shard_map/all_to_all | solution.py:198
  44.3 14.2 %collective-permute-start.5 = (f32[2,16,32,128]{3,2,1,0:T(8,128)S(1)}, f32[2,16,32,128]{3,2,1,0:T(8,128)S(1)}, u32[]{:S(2)}, u32[]{:S(2)}) collective-permute-start(f32[2,16,32,128]{3,2,1,0:T(8,128)S(1)} %get-tuple-element.18), channel_id=1, source_target_pairs={{0,24},{8,16},{16,8},{24,0},{1,25},{9,17},{17,9},{25,1},{2,26},{10... | collective-permute-start | bytes 1572872 | tf_op jit(solution)/shard_map/ppermute | solution.py:206
  45.3 24.5 %collective-permute-start.4 = (f32[2,16,32,128]{3,2,1,0:T(8,128)S(1)}, f32[2,16,32,128]{3,2,1,0:T(8,128)S(1)}, u32[]{:S(2)}, u32[]{:S(2)}) collective-permute-start(f32[2,16,32,128]{3,2,1,0:T(8,128)S(1)} %get-tuple-element.19), channel_id=1, source_target_pairs={{0,16},{8,24},{16,0},{24,8},{1,17},{9,25},{17,1},{25,9},{2,18},{10... | collective-permute-start | bytes 1572872 | tf_op jit(solution)/shard_map/ppermute | solution.py:206
  46.0 23.9 %collective-permute-start.3 = (f32[2,16,32,128]{3,2,1,0:T(8,128)S(1)}, f32[2,16,32,128]{3,2,1,0:T(8,128)S(1)}, u32[]{:S(2)}, u32[]{:S(2)}) collective-permute-start(f32[2,16,32,128]{3,2,1,0:T(8,128)S(1)} %get-tuple-element.20), channel_id=1, source_target_pairs={{0,8},{8,0},{16,24},{24,16},{1,9},{9,1},{17,25},{25,17},{2,10},{10... | collective-permute-start | bytes 1572872 | tf_op jit(solution)/shard_map/ppermute | solution.py:206
  76.4 19.8 %copy-start.6 = (bf16[256,256]{1,0:T(8,128)(2,1)S(1)}, bf16[256,256]{1,0:T(8,128)(2,1)}, u32[]{:S(2)}) copy-start(bf16[256,256]{1,0:T(8,128)(2,1)} %constant.74.clone.il.ll) | copy-start | bytes 393220
  76.4 19.8 %copy-start.7 = (bf16[256,256]{1,0:T(8,128)(2,1)S(1)}, bf16[256,256]{1,0:T(8,128)(2,1)}, u32[]{:S(2)}) copy-start(bf16[256,256]{1,0:T(8,128)(2,1)} %constant.73.clone.ih.lh) | copy-start | bytes 393220
  91.0 52.2 %all-to-all-start = ((f32[8,2,16,16,128]{4,3,2,1,0:T(8,128)}), f32[8,2,16,16,128]{4,3,2,1,0:T(8,128)}, u32[]{:S(2)}, u32[]{:S(2)}) async-start(f32[8,2,16,16,128]{4,3,2,1,0:T(8,128)} %copy-done.2), calls=%async_computation | async-start | bytes 4194304 | tf_op jit(solution)/shard_map/all_to_all | solution.py:198
  143.2 52.0 %all-to-all-start.3 = ((f32[8,2,16,16,128]{4,3,2,1,0:T(8,128)}), f32[8,2,16,16,128]{4,3,2,1,0:T(8,128)S(1)}, u32[]{:S(2)}, u32[]{:S(2)}) async-start(f32[8,2,16,16,128]{4,3,2,1,0:T(8,128)} %copy-done.5), calls=%async_computation.3 | async-start | bytes 4194304 | tf_op jit(solution)/shard_map/all_to_all | solution.py:198
  151.6 48.8 %copy-start.11 = (bf16[256,256]{1,0:T(8,128)(2,1)S(1)}, bf16[256,256]{1,0:T(8,128)(2,1)}, u32[]{:S(2)}) copy-start(bf16[256,256]{1,0:T(8,128)(2,1)} %constant.76.clone.rl) | copy-start | bytes 393220
  151.6 48.8 %copy-start.12 = (bf16[256,256]{1,0:T(8,128)(2,1)S(1)}, bf16[256,256]{1,0:T(8,128)(2,1)}, u32[]{:S(2)}) copy-start(bf16[256,256]{1,0:T(8,128)(2,1)} %constant.75.clone.rh) | copy-start | bytes 393220
  196.6 52.1 %all-to-all-start.1 = ((f32[8,2,16,16,128]{4,3,2,1,0:T(8,128)}), f32[8,2,16,16,128]{4,3,2,1,0:T(8,128)S(1)}, u32[]{:S(2)}, u32[]{:S(2)}) async-start(f32[8,2,16,16,128]{4,3,2,1,0:T(8,128)} %shard_map.140), calls=%async_computation.1 | async-start | bytes 4194304 | tf_op jit(solution)/shard_map/all_to_all | solution.py:198
  200.3 1.6 copy-start.4
  208.1 47.5 %collective-permute-start.11 = (f32[2,16,32,128]{3,2,1,0:T(8,128)}, f32[2,16,32,128]{3,2,1,0:T(8,128)}, u32[]{:S(2)}, u32[]{:S(2)}) collective-permute-start(f32[2,16,32,128]{3,2,1,0:T(8,128)} %get-tuple-element.26), channel_id=1, source_target_pairs={{0,24},{8,16},{16,8},{24,0},{1,25},{9,17},{17,9},{25,1},{2,26},{10... | collective-permute-start | bytes 1572872 | tf_op jit(solution)/shard_map/ppermute | solution.py:206
  209.0 46.8 %collective-permute-start.10 = (f32[2,16,32,128]{3,2,1,0:T(8,128)}, f32[2,16,32,128]{3,2,1,0:T(8,128)}, u32[]{:S(2)}, u32[]{:S(2)}) collective-permute-start(f32[2,16,32,128]{3,2,1,0:T(8,128)} %get-tuple-element.27), channel_id=1, source_target_pairs={{0,16},{8,24},{16,0},{24,8},{1,17},{9,25},{17,1},{25,9},{2,18},{10... | collective-permute-start | bytes 1572872 | tf_op jit(solution)/shard_map/ppermute | solution.py:206
  209.7 46.2 %collective-permute-start.9 = (f32[2,16,32,128]{3,2,1,0:T(8,128)}, f32[2,16,32,128]{3,2,1,0:T(8,128)}, u32[]{:S(2)}, u32[]{:S(2)}) collective-permute-start(f32[2,16,32,128]{3,2,1,0:T(8,128)} %get-tuple-element.28), channel_id=1, source_target_pairs={{0,8},{8,0},{16,24},{24,16},{1,9},{9,1},{17,25},{25,17},{2,10},{10... | collective-permute-start | bytes 1572872 | tf_op jit(solution)/shard_map/ppermute | solution.py:206
  253.7 3.9 %copy-start.10 = (f32[16,32,128]{2,1,0:T(8,128)S(1)}, f32[16,32,128]{2,1,0:T(8,128)}, u32[]{:S(2)}) copy-start(f32[16,32,128]{2,1,0:T(8,128)} %pot.3) | copy-start | bytes 786436
  253.9 14.2 %collective-permute-start.8 = (f32[2,16,32,128]{3,2,1,0:T(8,128)S(1)}, f32[2,16,32,128]{3,2,1,0:T(8,128)S(1)}, u32[]{:S(2)}, u32[]{:S(2)}) collective-permute-start(f32[2,16,32,128]{3,2,1,0:T(8,128)S(1)} %get-tuple-element.30), channel_id=1, source_target_pairs={{0,24},{8,16},{16,8},{24,0},{1,25},{9,17},{17,9},{25,1},{2,26},{10... | collective-permute-start | bytes 1572872 | tf_op jit(solution)/shard_map/ppermute | solution.py:206
  254.1 25.3 %collective-permute-start.7 = (f32[2,16,32,128]{3,2,1,0:T(8,128)S(1)}, f32[2,16,32,128]{3,2,1,0:T(8,128)S(1)}, u32[]{:S(2)}, u32[]{:S(2)}) collective-permute-start(f32[2,16,32,128]{3,2,1,0:T(8,128)S(1)} %get-tuple-element.31), channel_id=1, source_target_pairs={{0,16},{8,24},{16,0},{24,8},{1,17},{9,25},{17,1},{25,9},{2,18},{10... | collective-permute-start | bytes 1572872 | tf_op jit(solution)/shard_map/ppermute | solution.py:206
  255.7 23.8 %collective-permute-start.6 = (f32[2,16,32,128]{3,2,1,0:T(8,128)S(1)}, f32[2,16,32,128]{3,2,1,0:T(8,128)S(1)}, u32[]{:S(2)}, u32[]{:S(2)}) collective-permute-start(f32[2,16,32,128]{3,2,1,0:T(8,128)S(1)} %get-tuple-element.32), channel_id=1, source_target_pairs={{0,8},{8,0},{16,24},{24,16},{1,9},{9,1},{17,25},{25,17},{2,10},{10... | collective-permute-start | bytes 1572872 | tf_op jit(solution)/shard_map/ppermute | solution.py:206
  255.9 2.7 copy-start
  279.7 20.6 %copy-start.15 = (s32[8]{0:T(128)S(1)}, s32[8]{0:T(128)}, u32[]{:S(2)}) copy-start(s32[8]{0:T(128)} %param.15) | copy-start | bytes 100
  (8 other events, 9.3 us)

commit v3 on v2

--- a/solution.py
+++ b/solution.py
@@ -44,9 +44,50 @@
     return dot(vh, high) + (dot(vl, high) + dot(vh, low))
 
 
-def planes_kernel(order, lh, ll, rh, rl, src, dst):
-    pieces, _, depth, rows, n = src.shape
-    owners, width = dst.shape[0], dst.shape[3]
+def packing(n, owners):
+    limit = n * n // 4
+    signed = [k if k < n // 2 else k - n for k in range(n)]
+    reach = [math.isqrt(limit - f * f) for f in signed]
+    free, pairs = set(range(n)), []
+    for tail in sorted(range(n), key=lambda k: reach[k]):
+        fits = [k for k in free if k != tail and reach[k] + reach[tail] < n // 2]
+        if tail in free and fits:
+            host = max(fits, key=lambda k: reach[k])
+            pairs.append((host, tail))
+            free -= {host, tail}
+    count = max(c for c in range(0, len(pairs) + 1, 8) if (n - c) % owners == 0)
+    pairs = pairs[:count]
+    used = {k for pair in pairs for k in pair}
+    hosts, tails = [h for h, _ in pairs], [t for _, t in pairs]
+    order = [k for k in range(n) if k not in used] + hosts + tails
+    rows = n - count
+    f = np.array(signed)
+    square = (f[order[:rows], None] ** 2 + f[None, :] ** 2).astype(np.int32)
+    own = np.ones((max(count, 8), n), np.int32)
+    for i, (host, tail) in enumerate(pairs):
+        lane = np.arange(n)
+        own[i] = (lane <= reach[host]) | (lane >= n - reach[host])
+        other = f[tail] ** 2 + np.roll(f, n // 2) ** 2
+        square[rows - count + i] = np.where(own[i], square[rows - count + i], other)
+    return np.array(order), rows, square, own
+
+
+def gather_planes(planes):
+    depth, n = len(planes), planes[0].shape[0]
+    return lambda along: jnp.concatenate(
+        [
+            jnp.concatenate([along[z * n : (z + 1) * n, :n], along[z * n : (z + 1) * n, n:]], axis=0)
+            for z in range(depth)
+        ],
+        axis=1,
+    )
+
+
+def forward_kernel(order, lh, ll, rh, rl, own, src, dst):
+    pieces, _, depth, _, n = src.shape
+    owners, _, share, _, _ = dst.shape
+    rows = owners * share
+    count = n - rows
     planes = []
     for z in range(depth):
         part = [
@@ -55,54 +96,72 @@
         ]
         planes.append(jnp.concatenate(part, axis=1))
     along_x = right_apply(jnp.concatenate(planes, axis=0), rh[...], rl[...])
+    out = left_apply(lh[...], ll[...], gather_planes(planes)(along_x))
+    for q in range(2):
+        packed = []
+        for z in range(depth):
+            plane = out[q * n : (q + 1) * n, z * n : (z + 1) * n]
+            if count:
+                tail = pltpu.roll(plane[rows:], n // 2, 1)
+                host = jnp.where(own[...] != 0, plane[rows - count : rows], tail)
+                plane = jnp.concatenate([plane[: rows - count], host], axis=0)
+            packed.append(plane)
+        packed = jnp.swapaxes(jnp.stack(packed, axis=0), 0, 1)
+        dst[:, q] = packed.reshape(owners, share, depth, n)
+
+
+def inverse_kernel(order, lh, ll, rh, rl, own, src, dst):
+    owners, _, share, depth, n = src.shape
+    pieces, _, _, width, _ = dst.shape
+    rows = owners * share
+    count = n - rows
+    parts = [jnp.swapaxes(src[:, p].reshape(rows, depth, n), 0, 1) for p in range(2)]
+    planes = []
+    for z in range(depth):
+        part = []
+        for p in range(2):
+            plane = parts[p][z]
+            if count:
+                last = plane[rows - count :]
+                host = jnp.where(own[...] != 0, last, 0.0)
+                tail = pltpu.roll(jnp.where(own[...] != 0, 0.0, last), n // 2, 1)
+                plane = jnp.concatenate([plane[: rows - count], host, tail], axis=0)
+            part.append(plane)
+        planes.append(jnp.concatenate(part, axis=1))
+    along_x = right_apply(jnp.concatenate(planes, axis=0), rh[...], rl[...])
+    out = left_apply(lh[...], ll[...], gather_planes(planes)(along_x))
+    for z in range(depth):
+        for q in range(2):
+            for d in range(pieces):
+                first = q * n + d * width
+                dst[d ^ order[1], q, z] = out[first : first + width, z * n : (z + 1) * n]
+
+
+def middle_kernel(cutoff, squares, fh, fl, ih, il, src, dst):
+    owners, _, width, depth, n = src.shape
     columns = jnp.concatenate(
         [
-            jnp.concatenate(
-                [along_x[z * n : (z + 1) * n, :n], along_x[z * n : (z + 1) * n, n:]], axis=0
-            )
-            for z in range(depth)
+            jnp.concatenate([src[:, q, j].reshape(owners * depth, n) for q in range(2)], axis=0)
+            for j in range(width)
         ],
         axis=1,
     )
-    out = left_apply(lh[...], ll[...], columns)
-    for z in range(depth):
-        for q in range(2):
-            for d in range(owners):
-                first = q * n + d * width
-                dst[d ^ order[1], q, z] = out[first : first + width, z * n : (z + 1) * n]
-
-
-def middle_kernel(scalars, fh, fl, ih, il, src, dst):
-    owners, _, depth, width, n = src.shape
-    planes = []
-    for q in range(2):
-        planes.append(jnp.swapaxes(src[:, q].reshape(owners * depth, width, n), 0, 1))
-    columns = jnp.concatenate(
-        [jnp.concatenate([planes[0][j], planes[1][j]], axis=0) for j in range(width)], axis=1
-    )
     spectrum = left_apply(fh[...], fl[...], columns)
     kz = lax.broadcasted_iota(jnp.int32, (n, n), 0)
-    kx = lax.broadcasted_iota(jnp.int32, (n, n), 1)
     kz = jnp.where(kz < n // 2, kz, kz - n)
-    kx = jnp.where(kx < n // 2, kx, kx - n)
-    base = kz * kz + kx * kx
-    cutoff = scalars[0]
-    start = scalars[1] + pl.program_id(0) * width
+    base = kz * kz
     kinetic = []
     for j in range(width):
-        ky = start + j
-        ky = jnp.where(ky < n // 2, ky, ky - n)
-        total = base + ky * ky
+        total = base + squares[j]
         value = (0.5 * (math.pi / n) ** 2) * total.astype(F32)
-        kinetic.append(jnp.where(total <= cutoff, value, 0.0))
+        kinetic.append(jnp.where(total <= cutoff[0], value, 0.0))
     kinetic = jnp.concatenate(kinetic, axis=1)
     kinetic = jnp.concatenate([kinetic, kinetic], axis=0)
     back = left_apply(ih[...], il[...], spectrum * kinetic)
     for q in range(2):
-        stacked = jnp.stack(
-            [back[q * n : (q + 1) * n, j * n : (j + 1) * n] for j in range(width)], axis=0
-        )
-        dst[:, q] = jnp.swapaxes(stacked, 0, 1).reshape(owners, depth, width, n)
+        for j in range(width):
+            plane = back[q * n : (q + 1) * n, j * n : (j + 1) * n]
+            dst[:, q, j] = plane.reshape(owners, depth, n)
 
 
 def whole(shape):
@@ -112,37 +171,45 @@
 PARAMS = dict(dimension_semantics=("arbitrary",), vmem_limit_bytes=40 * 1024 * 1024)
 
 
-def planes_call(order, left, right, src, out_shape):
-    depth = math.gcd(src.shape[2], 4)
+def planes_call(kernel, order, left, right, own, src, out_shape, depths):
     n = src.shape[4]
-
-    def spec(shape):
-        return pl.BlockSpec((shape[0], 2, depth, shape[3], n), lambda i: (0, 0, i, 0, 0))
+    depth = math.gcd(src.shape[depths[0]], 8)
+
+    def spec(shape, axis):
+        block = shape[:axis] + (depth,) + shape[axis + 1 :]
+        return pl.BlockSpec(block, lambda i: tuple(i if a == axis else 0 for a in range(5)))
 
     table = whole((2 * n, 2 * n))
     return pl.pallas_call(
-        planes_kernel,
-        grid=(src.shape[2] // depth,),
-        in_specs=[pl.BlockSpec(memory_space=pltpu.SMEM)] + [table] * 4 + [spec(src.shape)],
-        out_specs=spec(out_shape),
+        kernel,
+        grid=(src.shape[depths[0]] // depth,),
+        in_specs=[pl.BlockSpec(memory_space=pltpu.SMEM)]
+        + [table] * 4
+        + [whole(own.shape), spec(src.shape, depths[0])],
+        out_specs=spec(out_shape, depths[1]),
         out_shape=jax.ShapeDtypeStruct(out_shape, F32),
         compiler_params=pltpu.CompilerParams(**PARAMS),
-    )(order, *left, *right, src)
-
-
-def middle_call(scalars, forward, inverse, src):
-    owners, _, depth, rows, n = src.shape
-    width = min(8, rows)
-    block = pl.BlockSpec((owners, 2, depth, width, n), lambda i: (0, 0, 0, i, 0))
+    )(order, *left, *right, own, src)
+
+
+def middle_call(cutoff, squares, forward, inverse, src):
+    owners, _, rows, depth, n = src.shape
+    width = max(w for w in range(1, 9) if rows % w == 0)
+    block = pl.BlockSpec((owners, 2, width, depth, n), lambda i: (0, 0, i, 0, 0))
     table = whole((2 * n, 2 * n))
     return pl.pallas_call(
         middle_kernel,
         grid=(rows // width,),
-        in_specs=[pl.BlockSpec(memory_space=pltpu.SMEM)] + [table] * 4 + [block],
+        in_specs=[
+            pl.BlockSpec(memory_space=pltpu.SMEM),
+            pl.BlockSpec((width, 1, n), lambda i: (i, 0, 0)),
+        ]
+        + [table] * 4
+        + [block],
         out_specs=block,
         out_shape=jax.ShapeDtypeStruct(src.shape, F32),
         compiler_params=pltpu.CompilerParams(**PARAMS),
-    )(scalars, *forward, *inverse, src)
+    )(cutoff, squares, *forward, *inverse, src)
 
 
 def finish_kernel(me, kin, wave, pot, *refs):
@@ -230,8 +297,13 @@
     fwd, inv = (fh, fl), (ih, il)
     fwd_t = (np.ascontiguousarray(fh.T), np.ascontiguousarray(fl.T))
     inv_t = (np.ascontiguousarray(ih.T), np.ascontiguousarray(il.T))
-    share = n // size_z
-    scalars = jnp.stack([cutoff_sq[0], (lax.axis_index("pz") * share).astype(jnp.int32)])
+    order, rows, square, own = packing(n, size_z)
+    share = rows // size_z
+    both = np.concatenate([order, n + order])
+    fwd_y, inv_y = (fh[both], fl[both]), (ih[:, both], il[:, both])
+    squares = lax.dynamic_slice_in_dim(
+        jnp.asarray(square)[:, None, :], lax.axis_index("pz") * share, share, 0
+    )
     me = lax.axis_index("py").astype(jnp.int32)
     there, back = jnp.stack([me, 0 * me]), jnp.stack([0 * me, me])
     spectra = []
@@ -247,11 +319,21 @@
         ]
         gathered = swap(sent, "py")
         spectra.append(gathered)
-    pieces = [planes_call(there, fwd, fwd_t, x, (size_z, 2, rows_z, share, n)) for x in spectra]
+    pieces = [
+        planes_call(
+            forward_kernel, there, fwd_y, fwd_t, own, x, (size_z, 2, share, rows_z, n), (2, 3)
+        )
+        for x in spectra
+    ]
     pieces = [exchange(piece, "pz") for piece in pieces]
-    pieces = [middle_call(scalars, fwd, inv, x) for x in pieces]
+    pieces = [middle_call(cutoff_sq, squares, fwd, inv, x) for x in pieces]
     pieces = [exchange(piece, "pz") for piece in pieces]
-    pieces = [planes_call(back, inv, inv_t, x, (size_y, 2, rows_z, rows_y, n)) for x in pieces]
+    pieces = [
+        planes_call(
+            inverse_kernel, back, inv_y, inv_t, own, x, (size_y, 2, rows_z, rows_y, n), (3, 2)
+        )
+        for x in pieces
+    ]
     applied, stats = None, []
     for index, piece in enumerate(pieces):
         kinetic_part = swap([piece[d] for d in range(size_y)], "py")

time: 301 us -> 277 us (0.920)
  waiting for transfers between devices: 204 us -> 183 us
  Pallas kernels: 34.5 us -> 31.3 us
    all_to_all x4, waiting for transfers between devices: 140 us -> 119 us  [exchange(): return lax.all_to_all(value, axis, split_axis=0, concat_axis=0, tiled=True)]
    unnamed x32 -> x40, local copies, waits for them, and re-layouts: 8.71 us -> 7.06 us
  transfers between devices with their start and end apart: 16 -> 16, of which waited for: 10 -> 10; matrix products, arithmetic and copies ran while one was open for 2% -> 2% of each run, Pallas kernels for 9% -> 8%
where the time goes in v3:
time: 277 us; the launch traced here: 276 us
  waiting for transfers between devices  183 us (66%)
  Pallas kernels  31.3 us (11%)
  starting transfers between devices  27.2 us (10%)
  blocking collectives  16.4 us (6%)
  local copies, waits for them, and re-layouts  12.8 us (5%)
  other arithmetic  3.64 us (1%)
    all_to_all x4, waiting for transfers between devices, exchange(): return lax.all_to_all(value, axis, split_axis=0, concat_axis=0, tiled=True)  119 us
    ppermute x12, waiting for transfers between devices, swap(): lax.ppermute(pieces[d], axis, [(i, i ^ d) for i in range(size)])  64.3 us
    pallas_call x4, Pallas kernels, planes_call(): pl.pallas_call(kernel, grid=(src.shape[depths[0]] // depth,), in_specs=[p...  18.9 us
    all_to_all x4, starting transfers between devices, exchange(): return lax.all_to_all(value, axis, split_axis=0, concat_axis=0, tiled=True)  18.3 us
    all_to_all x2, blocking collectives, exchange(): return lax.all_to_all(value, axis, split_axis=0, concat_axis=0, tiled=True)  16.4 us
    ppermute x12, starting transfers between devices, swap(): lax.ppermute(pieces[d], axis, [(i, i ^ d) for i in range(size)])  8.89 us
    unnamed x40, local copies, waits for them, and re-layouts  7.06 us
    pallas_call x2, Pallas kernels, finish_call(): pl.pallas_call(finish_kernel, grid_spec=pltpu.PrefetchScalarGridSpec(num_...  6.5 us
  transfers between devices with their start and end apart: 16, of which 10 were waited for; matrix products, arithmetic and copies ran while one was open for 2% of the time, Pallas kernels for 8%

profile of v3, /device:TPU:0, one launch (start us, length us, event | category | flops | bytes accessed | tf_op | source)
XLA Modules:
  0.0 276.4 jit_solution(10772879966762767410)
XLA Ops:
  2.4 2.5 collective-permute-start.2
  5.6 11.6 %collective-permute-done.2 = f32[2,16,32,128]{3,2,1,0:T(8,128)S(1)} collective-permute-done((f32[2,16,32,128]{3,2,1,0:T(8,128)S(1)}, f32[2,16,32,128]{3,2,1,0:T(8,128)S(1)}, u32[]{:S(2)}, u32[]{:S(2)}) %collective-permute-start.2) | collective-permute-done | bytes 524320 | tf_op jit(solution)/shard_map/ppermute | solution.py:273
  17.2 11.4 %collective-permute-done.1 = f32[2,16,32,128]{3,2,1,0:T(8,128)S(1)} collective-permute-done((f32[2,16,32,128]{3,2,1,0:T(8,128)S(1)}, f32[2,16,32,128]{3,2,1,0:T(8,128)S(1)}, u32[]{:S(2)}, u32[]{:S(2)}) %collective-permute-start.1) | collective-permute-done | bytes 524320 | tf_op jit(solution)/shard_map/ppermute | solution.py:273
  29.7 5.2 %shard_map.196 = f32[8,2,14,16,128]{4,3,2,1,0:T(8,128)} custom-call(s32[2]{0:T(128)S(1)} %pad_add_fusion.1.order, bf16[256,256]{1,0:T(8,128)(2,1)S(1)} %copy-done.17, bf16[256,256]{1,0:T(8,128)(2,1)S(1)} %copy-done.16, bf16[256,256]{1,0:T(8,128)(2,1)S(1)} %copy-done.15, bf16[256,256]{1,0:T(8,128)(2,1)S(1)} %copy-done.14, s32[16,128]{1,0:T(8,128)S(1)} %copy-done.18, ...), custom_call_target="tpu_custom_call" | custom-call | tf_op jit(solution)/shard_map/pallas_call | solution.py:183
  34.9 6.6 %all-to-all-start.2 = ((f32[8,2,14,16,128]{4,3,2,1,0:T(8,128)}), f32[8,2,14,16,128]{4,3,2,1,0:T(8,128)S(1)}, u32[]{:S(2)}, u32[]{:S(2)}) async-start(f32[8,2,14,16,128]{4,3,2,1,0:T(8,128)} %shard_map.196), calls=%async_computation.2 | async-start | bytes 3670016 | tf_op jit(solution)/shard_map/all_to_all | solution.py:265
  45.1 12.3 %collective-permute-done.5 = f32[2,16,32,128]{3,2,1,0:T(8,128)S(1)} collective-permute-done((f32[2,16,32,128]{3,2,1,0:T(8,128)S(1)}, f32[2,16,32,128]{3,2,1,0:T(8,128)S(1)}, u32[]{:S(2)}, u32[]{:S(2)}) %collective-permute-start.5) | collective-permute-done | bytes 524320 | tf_op jit(solution)/shard_map/ppermute | solution.py:273
  57.4 11.3 %collective-permute-done.4 = f32[2,16,32,128]{3,2,1,0:T(8,128)S(1)} collective-permute-done((f32[2,16,32,128]{3,2,1,0:T(8,128)S(1)}, f32[2,16,32,128]{3,2,1,0:T(8,128)S(1)}, u32[]{:S(2)}, u32[]{:S(2)}) %collective-permute-start.4) | collective-permute-done | bytes 524320 | tf_op jit(solution)/shard_map/ppermute | solution.py:273
  68.9 5.2 %shard_map.193 = f32[8,2,14,16,128]{4,3,2,1,0:T(8,128)} custom-call(s32[2]{0:T(128)S(1)} %pad_add_fusion.1.order, bf16[256,256]{1,0:T(8,128)(2,1)S(1)} %copy-done.17, bf16[256,256]{1,0:T(8,128)(2,1)S(1)} %copy-done.16, bf16[256,256]{1,0:T(8,128)(2,1)S(1)} %copy-done.15, bf16[256,256]{1,0:T(8,128)(2,1)S(1)} %copy-done.14, s32[16,128]{1,0:T(8,128)S(1)} %copy-done.18, ...), custom_call_target="tpu_custom_call" | custom-call | tf_op jit(solution)/shard_map/pallas_call | solution.py:183
  74.1 10.2 %all-to-all-done.2.src = f32[8,2,14,16,128]{4,3,2,1,0:T(8,128)S(1)} async-done(((f32[8,2,14,16,128]{4,3,2,1,0:T(8,128)}), f32[8,2,14,16,128]{4,3,2,1,0:T(8,128)S(1)}, u32[]{:S(2)}, u32[]{:S(2)}) %all-to-all-start.2) | async-done | bytes 1835040 | tf_op jit(solution)/shard_map/all_to_all | solution.py:265
  84.3 4.3 %all-to-all-start = ((f32[8,2,14,16,128]{4,3,2,1,0:T(8,128)}), f32[8,2,14,16,128]{4,3,2,1,0:T(8,128)}, u32[]{:S(2)}, u32[]{:S(2)}) async-start(f32[8,2,14,16,128]{4,3,2,1,0:T(8,128)} %shard_map.193), calls=%async_computation | async-start | bytes 3670016 | tf_op jit(solution)/shard_map/all_to_all | solution.py:265
  93.7 37.1 %all-to-all-done.src = f32[8,2,14,16,128]{4,3,2,1,0:T(8,128)} async-done(((f32[8,2,14,16,128]{4,3,2,1,0:T(8,128)}), f32[8,2,14,16,128]{4,3,2,1,0:T(8,128)}, u32[]{:S(2)}, u32[]{:S(2)}) %all-to-all-start) | async-done | bytes 1835040 | tf_op jit(solution)/shard_map/all_to_all | solution.py:265
  130.9 3.6 %all-to-all-start.3 = ((f32[8,2,14,16,128]{4,3,2,1,0:T(8,128)}), f32[8,2,14,16,128]{4,3,2,1,0:T(8,128)S(1)}, u32[]{:S(2)}, u32[]{:S(2)}) async-start(f32[8,2,14,16,128]{4,3,2,1,0:T(8,128)} %copy-done.4), calls=%async_computation.3 | async-start | bytes 3670016 | tf_op jit(solution)/shard_map/all_to_all | solution.py:265
  134.5 3.5 %shard_map.194 = f32[8,2,14,16,128]{4,3,2,1,0:T(8,128)S(1)} custom-call(s32[1]{0:T(128)S(6)} %copy.32.cutoff, s32[14,1,128]{2,1,0:T(1,128)S(1)} %dynamic_slice.28.squares, bf16[256,256]{1,0:T(8,128)(2,1)S(1)} %copy-done.13, bf16[256,256]{1,0:T(8,128)(2,1)S(1)} %copy-done.12, bf16[256,256]{1,0:T(8,128)(2,1)S(1)} %copy-done.11, ...), custom_call_target="tpu_custom_call" | custom-call | tf_op jit(solution)/shard_map/pallas_call | solution.py:200
  139.2 38.1 %all-to-all-done.3.src = f32[8,2,14,16,128]{4,3,2,1,0:T(8,128)S(1)} async-done(((f32[8,2,14,16,128]{4,3,2,1,0:T(8,128)}), f32[8,2,14,16,128]{4,3,2,1,0:T(8,128)S(1)}, u32[]{:S(2)}, u32[]{:S(2)}) %all-to-all-start.3) | async-done | bytes 1835040 | tf_op jit(solution)/shard_map/all_to_all | solution.py:265
  178.5 3.8 %all-to-all-start.1 = ((f32[8,2,14,16,128]{4,3,2,1,0:T(8,128)}), f32[8,2,14,16,128]{4,3,2,1,0:T(8,128)S(1)}, u32[]{:S(2)}, u32[]{:S(2)}) async-start(f32[8,2,14,16,128]{4,3,2,1,0:T(8,128)} %copy-done.3), calls=%async_computation.1 | async-start | bytes 3670016 | tf_op jit(solution)/shard_map/all_to_all | solution.py:265
  183.9 4.3 %shard_map.198 = f32[4,2,16,32,128]{4,3,2,1,0:T(8,128)S(1)} custom-call(s32[2]{0:T(128)S(1)} %pad_add_fusion.order, bf16[256,256]{1,0:T(8,128)(2,1)S(1)} %copy-done.9, bf16[256,256]{1,0:T(8,128)(2,1)S(1)} %copy-done.8, bf16[256,256]{1,0:T(8,128)(2,1)S(1)} %copy-done.7, bf16[256,256]{1,0:T(8,128)(2,1)S(1)} %copy-done.6, s32[16,128]{1,0:T(8,128)S(1)} %copy-done.18, ...), custom_call_target="tpu_custom_call" | custom-call | tf_op jit(solution)/shard_map/pallas_call | solution.py:183
  191.3 33.8 %all-to-all-done.1.src = f32[8,2,14,16,128]{4,3,2,1,0:T(8,128)S(1)} async-done(((f32[8,2,14,16,128]{4,3,2,1,0:T(8,128)}), f32[8,2,14,16,128]{4,3,2,1,0:T(8,128)S(1)}, u32[]{:S(2)}, u32[]{:S(2)}) %all-to-all-start.1) | async-done | bytes 1835040 | tf_op jit(solution)/shard_map/all_to_all | solution.py:265
  225.0 4.3 %shard_map.195 = f32[4,2,16,32,128]{4,3,2,1,0:T(8,128)S(1)} custom-call(s32[2]{0:T(128)S(1)} %pad_add_fusion.order, bf16[256,256]{1,0:T(8,128)(2,1)S(1)} %copy-done.9, bf16[256,256]{1,0:T(8,128)(2,1)S(1)} %copy-done.8, bf16[256,256]{1,0:T(8,128)(2,1)S(1)} %copy-done.7, bf16[256,256]{1,0:T(8,128)(2,1)S(1)} %copy-done.6, s32[16,128]{1,0:T(8,128)S(1)} %copy-done.18, ...), custom_call_target="tpu_custom_call" | custom-call | tf_op jit(solution)/shard_map/pallas_call | solution.py:183
  234.1 3.2 %shard_map.199 = (f32[2,8,16,32,128]{4,3,2,1,0:T(8,128)}, f32[4,8,128]{2,1,0:T(8,128)S(1)}) custom-call(s32[1]{0:T(128)} %bitcast.me, f32[4,2,16,32,128]{4,3,2,1,0:T(8,128)S(1)} %pad_maximum_fusion.3.kin, f32[2,8,16,32,128]{4,3,2,1,0:T(8,128)S(1)} %copy-done, f32[16,32,128]{2,1,0:T(8,128)S(1)} %copy-done.5), custom_call_target="tpu_custom_call" | custom-call | tf_op jit(solution)/shard_map/pallas_call | solution.py:247
  237.4 6.3 %collective-permute-done.8 = f32[2,16,32,128]{3,2,1,0:T(8,128)S(1)} collective-permute-done((f32[2,16,32,128]{3,2,1,0:T(8,128)S(1)}, f32[2,16,32,128]{3,2,1,0:T(8,128)S(1)}, u32[]{:S(2)}, u32[]{:S(2)}) %collective-permute-start.8) | collective-permute-done | bytes 524320 | tf_op jit(solution)/shard_map/ppermute | solution.py:273
  243.7 11.4 %collective-permute-done.7 = f32[2,16,32,128]{3,2,1,0:T(8,128)S(1)} collective-permute-done((f32[2,16,32,128]{3,2,1,0:T(8,128)S(1)}, f32[2,16,32,128]{3,2,1,0:T(8,128)S(1)}, u32[]{:S(2)}, u32[]{:S(2)}) %collective-permute-start.7) | collective-permute-done | bytes 524320 | tf_op jit(solution)/shard_map/ppermute | solution.py:273
  255.3 3.3 %shard_map.200 = (f32[2,8,16,32,128]{4,3,2,1,0:T(8,128)}, f32[4,8,128]{2,1,0:T(8,128)S(1)}) custom-call(s32[1]{0:T(128)} %bitcast.me, f32[4,2,16,32,128]{4,3,2,1,0:T(8,128)S(1)} %pad_maximum_fusion.2.kin, f32[2,8,16,32,128]{4,3,2,1,0:T(8,128)S(1)} %copy-done, f32[16,32,128]{2,1,0:T(8,128)S(1)} %copy-done.5, ...), custom_call_target="tpu_custom_call", output_to_operand_aliasing={{0}: (4, {})} | custom-call | tf_op jit(solution)/shard_map/pallas_call | solution.py:247
  258.8 6.1 %all_to_all.30 = f32[4,3,8]{2,1,0:T(4,128)S(1)} all-to-all(f32[4,3,8]{2,1,0:T(4,128)S(1)} %broadcast_in_dim.37), channel_id=1, replica_groups=mesh['py'=4,'pz'=8] {'py'}, dimensions={0} | all-to-all | bytes 768 | tf_op jit(solution)/shard_map/all_to_all | solution.py:265
  265.0 10.3 %all_to_all.31 = f32[8,3,8]{2,1,0:T(4,128)S(1)} all-to-all(f32[8,3,8]{2,1,0:T(4,128)S(1)} %broadcast_in_dim.40), channel_id=1, replica_groups=mesh['py'=4,'pz'=8] {'pz'}, dimensions={0} | all-to-all | bytes 1536 | tf_op jit(solution)/shard_map/all_to_all | solution.py:265
  (85 shorter events, 25.3 us)
Async XLA Ops:
  2.4 14.8 %collective-permute-start.2 = (f32[2,16,32,128]{3,2,1,0:T(8,128)S(1)}, f32[2,16,32,128]{3,2,1,0:T(8,128)S(1)}, u32[]{:S(2)}, u32[]{:S(2)}) collective-permute-start(f32[2,16,32,128]{3,2,1,0:T(8,128)S(1)} %get-tuple-element.22), channel_id=1, source_target_pairs={{0,24},{8,16},{16,8},{24,0},{1,25},{9,17},{17,9},{25,1},{2,26},{10... | collective-permute-start | bytes 1572872 | tf_op jit(solution)/shard_map/ppermute | solution.py:273
  4.9 23.7 %collective-permute-start.1 = (f32[2,16,32,128]{3,2,1,0:T(8,128)S(1)}, f32[2,16,32,128]{3,2,1,0:T(8,128)S(1)}, u32[]{:S(2)}, u32[]{:S(2)}) collective-permute-start(f32[2,16,32,128]{3,2,1,0:T(8,128)S(1)} %get-tuple-element.23), channel_id=1, source_target_pairs={{0,16},{8,24},{16,0},{24,8},{1,17},{9,25},{17,1},{25,9},{2,18},{10... | collective-permute-start | bytes 1572872 | tf_op jit(solution)/shard_map/ppermute | solution.py:273
  5.5 23.1 %collective-permute-start = (f32[2,16,32,128]{3,2,1,0:T(8,128)S(1)}, f32[2,16,32,128]{3,2,1,0:T(8,128)S(1)}, u32[]{:S(2)}, u32[]{:S(2)}) collective-permute-start(f32[2,16,32,128]{3,2,1,0:T(8,128)S(1)} %get-tuple-element.24), channel_id=1, source_target_pairs={{0,8},{8,0},{16,24},{24,16},{1,9},{9,1},{17,25},{25,17},{2,10},{10... | collective-permute-start | bytes 1572872 | tf_op jit(solution)/shard_map/ppermute | solution.py:273
  34.9 49.4 %all-to-all-start.2 = ((f32[8,2,14,16,128]{4,3,2,1,0:T(8,128)}), f32[8,2,14,16,128]{4,3,2,1,0:T(8,128)S(1)}, u32[]{:S(2)}, u32[]{:S(2)}) async-start(f32[8,2,14,16,128]{4,3,2,1,0:T(8,128)} %shard_map.196), calls=%async_computation.2 | async-start | bytes 3670016 | tf_op jit(solution)/shard_map/all_to_all | solution.py:265
  43.2 14.2 %collective-permute-start.5 = (f32[2,16,32,128]{3,2,1,0:T(8,128)S(1)}, f32[2,16,32,128]{3,2,1,0:T(8,128)S(1)}, u32[]{:S(2)}, u32[]{:S(2)}) collective-permute-start(f32[2,16,32,128]{3,2,1,0:T(8,128)S(1)} %get-tuple-element.18), channel_id=1, source_target_pairs={{0,24},{8,16},{16,8},{24,0},{1,25},{9,17},{17,9},{25,1},{2,26},{10... | collective-permute-start | bytes 1572872 | tf_op jit(solution)/shard_map/ppermute | solution.py:273
  44.2 24.5 %collective-permute-start.4 = (f32[2,16,32,128]{3,2,1,0:T(8,128)S(1)}, f32[2,16,32,128]{3,2,1,0:T(8,128)S(1)}, u32[]{:S(2)}, u32[]{:S(2)}) collective-permute-start(f32[2,16,32,128]{3,2,1,0:T(8,128)S(1)} %get-tuple-element.19), channel_id=1, source_target_pairs={{0,16},{8,24},{16,0},{24,8},{1,17},{9,25},{17,1},{25,9},{2,18},{10... | collective-permute-start | bytes 1572872 | tf_op jit(solution)/shard_map/ppermute | solution.py:273
  44.8 23.9 %collective-permute-start.3 = (f32[2,16,32,128]{3,2,1,0:T(8,128)S(1)}, f32[2,16,32,128]{3,2,1,0:T(8,128)S(1)}, u32[]{:S(2)}, u32[]{:S(2)}) collective-permute-start(f32[2,16,32,128]{3,2,1,0:T(8,128)S(1)} %get-tuple-element.20), channel_id=1, source_target_pairs={{0,8},{8,0},{16,24},{24,16},{1,9},{9,1},{17,25},{25,17},{2,10},{10... | collective-permute-start | bytes 1572872 | tf_op jit(solution)/shard_map/ppermute | solution.py:273
  74.1 16.0 %copy-start.11 = (bf16[256,256]{1,0:T(8,128)(2,1)S(1)}, bf16[256,256]{1,0:T(8,128)(2,1)}, u32[]{:S(2)}) copy-start(bf16[256,256]{1,0:T(8,128)(2,1)} %constant.92.clone.ih) | copy-start | bytes 393220
  74.1 16.0 %copy-start.12 = (bf16[256,256]{1,0:T(8,128)(2,1)S(1)}, bf16[256,256]{1,0:T(8,128)(2,1)}, u32[]{:S(2)}) copy-start(bf16[256,256]{1,0:T(8,128)(2,1)} %constant.91.clone.fl) | copy-start | bytes 393220
  74.1 16.0 %copy-start.13 = (bf16[256,256]{1,0:T(8,128)(2,1)S(1)}, bf16[256,256]{1,0:T(8,128)(2,1)}, u32[]{:S(2)}) copy-start(bf16[256,256]{1,0:T(8,128)(2,1)} %constant.90.clone.fh) | copy-start | bytes 393220
  84.3 46.6 %all-to-all-start = ((f32[8,2,14,16,128]{4,3,2,1,0:T(8,128)}), f32[8,2,14,16,128]{4,3,2,1,0:T(8,128)}, u32[]{:S(2)}, u32[]{:S(2)}) async-start(f32[8,2,14,16,128]{4,3,2,1,0:T(8,128)} %shard_map.193), calls=%async_computation | async-start | bytes 3670016 | tf_op jit(solution)/shard_map/all_to_all | solution.py:265
  130.9 46.4 %all-to-all-start.3 = ((f32[8,2,14,16,128]{4,3,2,1,0:T(8,128)}), f32[8,2,14,16,128]{4,3,2,1,0:T(8,128)S(1)}, u32[]{:S(2)}, u32[]{:S(2)}) async-start(f32[8,2,14,16,128]{4,3,2,1,0:T(8,128)} %copy-done.4), calls=%async_computation.3 | async-start | bytes 3670016 | tf_op jit(solution)/shard_map/all_to_all | solution.py:265
  139.2 43.2 %copy-start.6 = (bf16[256,256]{1,0:T(8,128)(2,1)S(1)}, bf16[256,256]{1,0:T(8,128)(2,1)}, u32[]{:S(2)}) copy-start(bf16[256,256]{1,0:T(8,128)(2,1)} %constant.97.clone.rl) | copy-start | bytes 393220
  139.2 43.2 %copy-start.7 = (bf16[256,256]{1,0:T(8,128)(2,1)S(1)}, bf16[256,256]{1,0:T(8,128)(2,1)}, u32[]{:S(2)}) copy-start(bf16[256,256]{1,0:T(8,128)(2,1)} %constant.96.clone.rh) | copy-start | bytes 393220
  139.2 43.2 %copy-start.8 = (bf16[256,256]{1,0:T(8,128)(2,1)S(1)}, bf16[256,256]{1,0:T(8,128)(2,1)}, u32[]{:S(2)}) copy-start(bf16[256,256]{1,0:T(8,128)(2,1)} %constant.95.clone.ll) | copy-start | bytes 393220
  139.2 43.2 %copy-start.9 = (bf16[256,256]{1,0:T(8,128)(2,1)S(1)}, bf16[256,256]{1,0:T(8,128)(2,1)}, u32[]{:S(2)}) copy-start(bf16[256,256]{1,0:T(8,128)(2,1)} %constant.94.clone.lh) | copy-start | bytes 393220
  178.5 46.5 %all-to-all-start.1 = ((f32[8,2,14,16,128]{4,3,2,1,0:T(8,128)}), f32[8,2,14,16,128]{4,3,2,1,0:T(8,128)S(1)}, u32[]{:S(2)}, u32[]{:S(2)}) async-start(f32[8,2,14,16,128]{4,3,2,1,0:T(8,128)} %copy-done.3), calls=%async_computation.1 | async-start | bytes 3670016 | tf_op jit(solution)/shard_map/all_to_all | solution.py:265
  189.4 41.9 %collective-permute-start.11 = (f32[2,16,32,128]{3,2,1,0:T(8,128)}, f32[2,16,32,128]{3,2,1,0:T(8,128)}, u32[]{:S(2)}, u32[]{:S(2)}) collective-permute-start(f32[2,16,32,128]{3,2,1,0:T(8,128)} %get-tuple-element.26), channel_id=1, source_target_pairs={{0,24},{8,16},{16,8},{24,0},{1,25},{9,17},{17,9},{25,1},{2,26},{10... | collective-permute-start | bytes 1572872 | tf_op jit(solution)/shard_map/ppermute | solution.py:273
  190.2 41.3 %collective-permute-start.10 = (f32[2,16,32,128]{3,2,1,0:T(8,128)}, f32[2,16,32,128]{3,2,1,0:T(8,128)}, u32[]{:S(2)}, u32[]{:S(2)}) collective-permute-start(f32[2,16,32,128]{3,2,1,0:T(8,128)} %get-tuple-element.27), channel_id=1, source_target_pairs={{0,16},{8,24},{16,0},{24,8},{1,17},{9,25},{17,1},{25,9},{2,18},{10... | collective-permute-start | bytes 1572872 | tf_op jit(solution)/shard_map/ppermute | solution.py:273
  191.0 40.5 %collective-permute-start.9 = (f32[2,16,32,128]{3,2,1,0:T(8,128)S(1)}, f32[2,16,32,128]{3,2,1,0:T(8,128)}, u32[]{:S(2)}, u32[]{:S(2)}) collective-permute-start(f32[2,16,32,128]{3,2,1,0:T(8,128)S(1)} %get-tuple-element.28), channel_id=1, source_target_pairs={{0,8},{8,0},{16,24},{24,16},{1,9},{9,1},{17,25},{25,17},{2,10},{10... | collective-permute-start | bytes 1572872 | tf_op jit(solution)/shard_map/ppermute | solution.py:273
  229.5 14.2 %collective-permute-start.8 = (f32[2,16,32,128]{3,2,1,0:T(8,128)S(1)}, f32[2,16,32,128]{3,2,1,0:T(8,128)S(1)}, u32[]{:S(2)}, u32[]{:S(2)}) collective-permute-start(f32[2,16,32,128]{3,2,1,0:T(8,128)S(1)} %get-tuple-element.30), channel_id=1, source_target_pairs={{0,24},{8,16},{16,8},{24,0},{1,25},{9,17},{17,9},{25,1},{2,26},{10... | collective-permute-start | bytes 1572872 | tf_op jit(solution)/shard_map/ppermute | solution.py:273
  229.7 25.3 %collective-permute-start.7 = (f32[2,16,32,128]{3,2,1,0:T(8,128)S(1)}, f32[2,16,32,128]{3,2,1,0:T(8,128)S(1)}, u32[]{:S(2)}, u32[]{:S(2)}) collective-permute-start(f32[2,16,32,128]{3,2,1,0:T(8,128)S(1)} %get-tuple-element.31), channel_id=1, source_target_pairs={{0,16},{8,24},{16,0},{24,8},{1,17},{9,25},{17,1},{25,9},{2,18},{10... | collective-permute-start | bytes 1572872 | tf_op jit(solution)/shard_map/ppermute | solution.py:273
  231.3 23.8 %collective-permute-start.6 = (f32[2,16,32,128]{3,2,1,0:T(8,128)S(1)}, f32[2,16,32,128]{3,2,1,0:T(8,128)S(1)}, u32[]{:S(2)}, u32[]{:S(2)}) collective-permute-start(f32[2,16,32,128]{3,2,1,0:T(8,128)S(1)} %get-tuple-element.32), channel_id=1, source_target_pairs={{0,8},{8,0},{16,24},{24,16},{1,9},{9,1},{17,25},{25,17},{2,10},{10... | collective-permute-start | bytes 1572872 | tf_op jit(solution)/shard_map/ppermute | solution.py:273
  255.3 20.6 %copy-start.19 = (s32[8]{0:T(128)S(1)}, s32[8]{0:T(128)}, u32[]{:S(2)}) copy-start(s32[8]{0:T(128)} %param.21) | copy-start | bytes 100
  (12 other events, 32.8 us)

commit v4 on v3

--- a/solution.py
+++ b/solution.py
@@ -341,7 +341,7 @@
             me[None], kinetic_part, wavefunctions, potential, index * size_y, applied
         )
         stats.append(some[:, :3, 0])
-    total = merge(merge(jnp.concatenate(stats, axis=0).T, "py"), "pz")
+    total = merge(jnp.concatenate(stats, axis=0).T, ("py", "pz"))
     rayleigh = total[1] / total[0]
     residual_norm = jnp.sqrt(total[2] / total[0]) * (1.0 - locked_mask.astype(F32))
     return (applied, rayleigh, residual_norm)

time: 277 us -> 271 us (0.978)
  blocking collectives: 16.4 us -> 10.8 us
    all_to_all x2 -> x1, blocking collectives: 16.4 us -> 10.8 us  [exchange(): return lax.all_to_all(value, axis, split_axis=0, concat_axis=0, tiled=True)]
where the time goes in v4:
time: 271 us
  waiting for transfers between devices  184 us (68%)
  Pallas kernels  31.3 us (12%)
  starting transfers between devices  27.2 us (10%)
  local copies, waits for them, and re-layouts  12.8 us (5%)
  blocking collectives  10.8 us (4%)
  other arithmetic  3.57 us (1%)
    all_to_all x4, waiting for transfers between devices, exchange(): return lax.all_to_all(value, axis, split_axis=0, concat_axis=0, tiled=True)  119 us
    ppermute x12, waiting for transfers between devices, swap(): lax.ppermute(pieces[d], axis, [(i, i ^ d) for i in range(size)])  64.3 us
    pallas_call x4, Pallas kernels, planes_call(): pl.pallas_call(kernel, grid=(src.shape[depths[0]] // depth,), in_specs=[p...  18.9 us
    all_to_all x4, starting transfers between devices, exchange(): return lax.all_to_all(value, axis, split_axis=0, concat_axis=0, tiled=True)  18.3 us
    all_to_all x1, blocking collectives, exchange(): return lax.all_to_all(value, axis, split_axis=0, concat_axis=0, tiled=True)  10.8 us
    ppermute x12, starting transfers between devices, swap(): lax.ppermute(pieces[d], axis, [(i, i ^ d) for i in range(size)])  8.89 us
    unnamed x40, local copies, waits for them, and re-layouts  7.07 us
    pallas_call x2, Pallas kernels, finish_call(): pl.pallas_call(finish_kernel, grid_spec=pltpu.PrefetchScalarGridSpec(num_...  6.5 us
  transfers between devices with their start and end apart: 16, of which 10 were waited for; matrix products, arithmetic and copies ran while one was open for 2% of the time, Pallas kernels for 8%

profile of v4, /device:TPU:0, one launch (start us, length us, event | category | flops | bytes accessed | tf_op | source)
XLA Modules:
  0.0 270.8 jit_solution(16480160598825271359)
XLA Ops:
  2.4 2.5 collective-permute-start.2
  5.6 11.6 %collective-permute-done.2 = f32[2,16,32,128]{3,2,1,0:T(8,128)S(1)} collective-permute-done((f32[2,16,32,128]{3,2,1,0:T(8,128)S(1)}, f32[2,16,32,128]{3,2,1,0:T(8,128)S(1)}, u32[]{:S(2)}, u32[]{:S(2)}) %collective-permute-start.2) | collective-permute-done | bytes 524320 | tf_op jit(solution)/shard_map/ppermute | solution.py:273
  17.2 11.4 %collective-permute-done.1 = f32[2,16,32,128]{3,2,1,0:T(8,128)S(1)} collective-permute-done((f32[2,16,32,128]{3,2,1,0:T(8,128)S(1)}, f32[2,16,32,128]{3,2,1,0:T(8,128)S(1)}, u32[]{:S(2)}, u32[]{:S(2)}) %collective-permute-start.1) | collective-permute-done | bytes 524320 | tf_op jit(solution)/shard_map/ppermute | solution.py:273
  29.7 5.2 %shard_map.196 = f32[8,2,14,16,128]{4,3,2,1,0:T(8,128)} custom-call(s32[2]{0:T(128)S(1)} %pad_add_fusion.1.order, bf16[256,256]{1,0:T(8,128)(2,1)S(1)} %copy-done.17, bf16[256,256]{1,0:T(8,128)(2,1)S(1)} %copy-done.16, bf16[256,256]{1,0:T(8,128)(2,1)S(1)} %copy-done.15, bf16[256,256]{1,0:T(8,128)(2,1)S(1)} %copy-done.14, s32[16,128]{1,0:T(8,128)S(1)} %copy-done.18, ...), custom_call_target="tpu_custom_call" | custom-call | tf_op jit(solution)/shard_map/pallas_call | solution.py:183
  34.9 6.6 %all-to-all-start.2 = ((f32[8,2,14,16,128]{4,3,2,1,0:T(8,128)}), f32[8,2,14,16,128]{4,3,2,1,0:T(8,128)S(1)}, u32[]{:S(2)}, u32[]{:S(2)}) async-start(f32[8,2,14,16,128]{4,3,2,1,0:T(8,128)} %shard_map.196), calls=%async_computation.2 | async-start | bytes 3670016 | tf_op jit(solution)/shard_map/all_to_all | solution.py:265
  45.1 12.3 %collective-permute-done.5 = f32[2,16,32,128]{3,2,1,0:T(8,128)S(1)} collective-permute-done((f32[2,16,32,128]{3,2,1,0:T(8,128)S(1)}, f32[2,16,32,128]{3,2,1,0:T(8,128)S(1)}, u32[]{:S(2)}, u32[]{:S(2)}) %collective-permute-start.5) | collective-permute-done | bytes 524320 | tf_op jit(solution)/shard_map/ppermute | solution.py:273
  57.4 11.3 %collective-permute-done.4 = f32[2,16,32,128]{3,2,1,0:T(8,128)S(1)} collective-permute-done((f32[2,16,32,128]{3,2,1,0:T(8,128)S(1)}, f32[2,16,32,128]{3,2,1,0:T(8,128)S(1)}, u32[]{:S(2)}, u32[]{:S(2)}) %collective-permute-start.4) | collective-permute-done | bytes 524320 | tf_op jit(solution)/shard_map/ppermute | solution.py:273
  68.9 5.2 %shard_map.193 = f32[8,2,14,16,128]{4,3,2,1,0:T(8,128)} custom-call(s32[2]{0:T(128)S(1)} %pad_add_fusion.1.order, bf16[256,256]{1,0:T(8,128)(2,1)S(1)} %copy-done.17, bf16[256,256]{1,0:T(8,128)(2,1)S(1)} %copy-done.16, bf16[256,256]{1,0:T(8,128)(2,1)S(1)} %copy-done.15, bf16[256,256]{1,0:T(8,128)(2,1)S(1)} %copy-done.14, s32[16,128]{1,0:T(8,128)S(1)} %copy-done.18, ...), custom_call_target="tpu_custom_call" | custom-call | tf_op jit(solution)/shard_map/pallas_call | solution.py:183
  74.1 10.2 %all-to-all-done.2.src = f32[8,2,14,16,128]{4,3,2,1,0:T(8,128)S(1)} async-done(((f32[8,2,14,16,128]{4,3,2,1,0:T(8,128)}), f32[8,2,14,16,128]{4,3,2,1,0:T(8,128)S(1)}, u32[]{:S(2)}, u32[]{:S(2)}) %all-to-all-start.2) | async-done | bytes 1835040 | tf_op jit(solution)/shard_map/all_to_all | solution.py:265
  84.3 4.3 %all-to-all-start = ((f32[8,2,14,16,128]{4,3,2,1,0:T(8,128)}), f32[8,2,14,16,128]{4,3,2,1,0:T(8,128)}, u32[]{:S(2)}, u32[]{:S(2)}) async-start(f32[8,2,14,16,128]{4,3,2,1,0:T(8,128)} %shard_map.193), calls=%async_computation | async-start | bytes 3670016 | tf_op jit(solution)/shard_map/all_to_all | solution.py:265
  90.1 2.4 shard_map.197
  93.7 37.1 %all-to-all-done.src = f32[8,2,14,16,128]{4,3,2,1,0:T(8,128)} async-done(((f32[8,2,14,16,128]{4,3,2,1,0:T(8,128)}), f32[8,2,14,16,128]{4,3,2,1,0:T(8,128)}, u32[]{:S(2)}, u32[]{:S(2)}) %all-to-all-start) | async-done | bytes 1835040 | tf_op jit(solution)/shard_map/all_to_all | solution.py:265
  130.9 3.6 %all-to-all-start.3 = ((f32[8,2,14,16,128]{4,3,2,1,0:T(8,128)}), f32[8,2,14,16,128]{4,3,2,1,0:T(8,128)S(1)}, u32[]{:S(2)}, u32[]{:S(2)}) async-start(f32[8,2,14,16,128]{4,3,2,1,0:T(8,128)} %copy-done.4), calls=%async_computation.3 | async-start | bytes 3670016 | tf_op jit(solution)/shard_map/all_to_all | solution.py:265
  134.5 3.5 %shard_map.194 = f32[8,2,14,16,128]{4,3,2,1,0:T(8,128)S(1)} custom-call(s32[1]{0:T(128)S(6)} %copy.41.cutoff, s32[14,1,128]{2,1,0:T(1,128)S(1)} %dynamic_slice.28.squares, bf16[256,256]{1,0:T(8,128)(2,1)S(1)} %copy-done.13, bf16[256,256]{1,0:T(8,128)(2,1)S(1)} %copy-done.12, bf16[256,256]{1,0:T(8,128)(2,1)S(1)} %copy-done.11, ...), custom_call_target="tpu_custom_call" | custom-call | tf_op jit(solution)/shard_map/pallas_call | solution.py:200
  139.2 38.1 %all-to-all-done.3.src = f32[8,2,14,16,128]{4,3,2,1,0:T(8,128)S(1)} async-done(((f32[8,2,14,16,128]{4,3,2,1,0:T(8,128)}), f32[8,2,14,16,128]{4,3,2,1,0:T(8,128)S(1)}, u32[]{:S(2)}, u32[]{:S(2)}) %all-to-all-start.3) | async-done | bytes 1835040 | tf_op jit(solution)/shard_map/all_to_all | solution.py:265
  178.6 3.8 %all-to-all-start.1 = ((f32[8,2,14,16,128]{4,3,2,1,0:T(8,128)}), f32[8,2,14,16,128]{4,3,2,1,0:T(8,128)S(1)}, u32[]{:S(2)}, u32[]{:S(2)}) async-start(f32[8,2,14,16,128]{4,3,2,1,0:T(8,128)} %copy-done.3), calls=%async_computation.1 | async-start | bytes 3670016 | tf_op jit(solution)/shard_map/all_to_all | solution.py:265
  183.9 4.3 %shard_map.198 = f32[4,2,16,32,128]{4,3,2,1,0:T(8,128)S(1)} custom-call(s32[2]{0:T(128)S(1)} %pad_add_fusion.order, bf16[256,256]{1,0:T(8,128)(2,1)S(1)} %copy-done.9, bf16[256,256]{1,0:T(8,128)(2,1)S(1)} %copy-done.8, bf16[256,256]{1,0:T(8,128)(2,1)S(1)} %copy-done.7, bf16[256,256]{1,0:T(8,128)(2,1)S(1)} %copy-done.6, s32[16,128]{1,0:T(8,128)S(1)} %copy-done.18, ...), custom_call_target="tpu_custom_call" | custom-call | tf_op jit(solution)/shard_map/pallas_call | solution.py:183
  191.2 33.8 %all-to-all-done.1.src = f32[8,2,14,16,128]{4,3,2,1,0:T(8,128)S(1)} async-done(((f32[8,2,14,16,128]{4,3,2,1,0:T(8,128)}), f32[8,2,14,16,128]{4,3,2,1,0:T(8,128)S(1)}, u32[]{:S(2)}, u32[]{:S(2)}) %all-to-all-start.1) | async-done | bytes 1835040 | tf_op jit(solution)/shard_map/all_to_all | solution.py:265
  225.1 4.3 %shard_map.195 = f32[4,2,16,32,128]{4,3,2,1,0:T(8,128)S(1)} custom-call(s32[2]{0:T(128)S(1)} %pad_add_fusion.order, bf16[256,256]{1,0:T(8,128)(2,1)S(1)} %copy-done.9, bf16[256,256]{1,0:T(8,128)(2,1)S(1)} %copy-done.8, bf16[256,256]{1,0:T(8,128)(2,1)S(1)} %copy-done.7, bf16[256,256]{1,0:T(8,128)(2,1)S(1)} %copy-done.6, s32[16,128]{1,0:T(8,128)S(1)} %copy-done.18, ...), custom_call_target="tpu_custom_call" | custom-call | tf_op jit(solution)/shard_map/pallas_call | solution.py:183
  234.2 3.2 %shard_map.199 = (f32[2,8,16,32,128]{4,3,2,1,0:T(8,128)}, f32[4,8,128]{2,1,0:T(8,128)S(1)}) custom-call(s32[1]{0:T(128)} %bitcast.me, f32[4,2,16,32,128]{4,3,2,1,0:T(8,128)S(1)} %pad_maximum_fusion.3.kin, f32[2,8,16,32,128]{4,3,2,1,0:T(8,128)S(1)} %copy-done, f32[16,32,128]{2,1,0:T(8,128)S(1)} %copy-done.5), custom_call_target="tpu_custom_call" | custom-call | tf_op jit(solution)/shard_map/pallas_call | solution.py:247
  237.4 6.3 %collective-permute-done.8 = f32[2,16,32,128]{3,2,1,0:T(8,128)S(1)} collective-permute-done((f32[2,16,32,128]{3,2,1,0:T(8,128)S(1)}, f32[2,16,32,128]{3,2,1,0:T(8,128)S(1)}, u32[]{:S(2)}, u32[]{:S(2)}) %collective-permute-start.8) | collective-permute-done | bytes 524320 | tf_op jit(solution)/shard_map/ppermute | solution.py:273
  243.7 11.4 %collective-permute-done.7 = f32[2,16,32,128]{3,2,1,0:T(8,128)S(1)} collective-permute-done((f32[2,16,32,128]{3,2,1,0:T(8,128)S(1)}, f32[2,16,32,128]{3,2,1,0:T(8,128)S(1)}, u32[]{:S(2)}, u32[]{:S(2)}) %collective-permute-start.7) | collective-permute-done | bytes 524320 | tf_op jit(solution)/shard_map/ppermute | solution.py:273
  255.4 3.3 %shard_map.200 = (f32[2,8,16,32,128]{4,3,2,1,0:T(8,128)}, f32[4,8,128]{2,1,0:T(8,128)S(1)}) custom-call(s32[1]{0:T(128)} %bitcast.me, f32[4,2,16,32,128]{4,3,2,1,0:T(8,128)S(1)} %pad_maximum_fusion.2.kin, f32[2,8,16,32,128]{4,3,2,1,0:T(8,128)S(1)} %copy-done, f32[16,32,128]{2,1,0:T(8,128)S(1)} %copy-done.5, ...), custom_call_target="tpu_custom_call", output_to_operand_aliasing={{0}: (4, {})} | custom-call | tf_op jit(solution)/shard_map/pallas_call | solution.py:247
  258.8 10.8 %all_to_all.25 = f32[32,3,8]{2,1,0:T(4,128)S(1)} all-to-all(f32[32,3,8]{2,1,0:T(4,128)S(1)} %broadcast_in_dim.23), channel_id=1, replica_groups=mesh['py'=4,'pz'=8] {'py','pz'}, dimensions={0} | all-to-all | bytes 6144 | tf_op jit(solution)/shard_map/all_to_all | solution.py:265
  (79 shorter events, 22.8 us)
Async XLA Ops:
  2.4 14.8 %collective-permute-start.2 = (f32[2,16,32,128]{3,2,1,0:T(8,128)S(1)}, f32[2,16,32,128]{3,2,1,0:T(8,128)S(1)}, u32[]{:S(2)}, u32[]{:S(2)}) collective-permute-start(f32[2,16,32,128]{3,2,1,0:T(8,128)S(1)} %get-tuple-element.20), channel_id=1, source_target_pairs={{0,24},{8,16},{16,8},{24,0},{1,25},{9,17},{17,9},{25,1},{2,26},{10... | collective-permute-start | bytes 1572872 | tf_op jit(solution)/shard_map/ppermute | solution.py:273
  4.9 23.7 %collective-permute-start.1 = (f32[2,16,32,128]{3,2,1,0:T(8,128)S(1)}, f32[2,16,32,128]{3,2,1,0:T(8,128)S(1)}, u32[]{:S(2)}, u32[]{:S(2)}) collective-permute-start(f32[2,16,32,128]{3,2,1,0:T(8,128)S(1)} %get-tuple-element.21), channel_id=1, source_target_pairs={{0,16},{8,24},{16,0},{24,8},{1,17},{9,25},{17,1},{25,9},{2,18},{10... | collective-permute-start | bytes 1572872 | tf_op jit(solution)/shard_map/ppermute | solution.py:273
  5.5 23.1 %collective-permute-start = (f32[2,16,32,128]{3,2,1,0:T(8,128)S(1)}, f32[2,16,32,128]{3,2,1,0:T(8,128)S(1)}, u32[]{:S(2)}, u32[]{:S(2)}) collective-permute-start(f32[2,16,32,128]{3,2,1,0:T(8,128)S(1)} %get-tuple-element.22), channel_id=1, source_target_pairs={{0,8},{8,0},{16,24},{24,16},{1,9},{9,1},{17,25},{25,17},{2,10},{10... | collective-permute-start | bytes 1572872 | tf_op jit(solution)/shard_map/ppermute | solution.py:273
  34.9 49.4 %all-to-all-start.2 = ((f32[8,2,14,16,128]{4,3,2,1,0:T(8,128)}), f32[8,2,14,16,128]{4,3,2,1,0:T(8,128)S(1)}, u32[]{:S(2)}, u32[]{:S(2)}) async-start(f32[8,2,14,16,128]{4,3,2,1,0:T(8,128)} %shard_map.196), calls=%async_computation.2 | async-start | bytes 3670016 | tf_op jit(solution)/shard_map/all_to_all | solution.py:265
  43.2 14.2 %collective-permute-start.5 = (f32[2,16,32,128]{3,2,1,0:T(8,128)S(1)}, f32[2,16,32,128]{3,2,1,0:T(8,128)S(1)}, u32[]{:S(2)}, u32[]{:S(2)}) collective-permute-start(f32[2,16,32,128]{3,2,1,0:T(8,128)S(1)} %get-tuple-element.16), channel_id=1, source_target_pairs={{0,24},{8,16},{16,8},{24,0},{1,25},{9,17},{17,9},{25,1},{2,26},{10... | collective-permute-start | bytes 1572872 | tf_op jit(solution)/shard_map/ppermute | solution.py:273
  44.2 24.5 %collective-permute-start.4 = (f32[2,16,32,128]{3,2,1,0:T(8,128)S(1)}, f32[2,16,32,128]{3,2,1,0:T(8,128)S(1)}, u32[]{:S(2)}, u32[]{:S(2)}) collective-permute-start(f32[2,16,32,128]{3,2,1,0:T(8,128)S(1)} %get-tuple-element.17), channel_id=1, source_target_pairs={{0,16},{8,24},{16,0},{24,8},{1,17},{9,25},{17,1},{25,9},{2,18},{10... | collective-permute-start | bytes 1572872 | tf_op jit(solution)/shard_map/ppermute | solution.py:273
  44.9 23.9 %collective-permute-start.3 = (f32[2,16,32,128]{3,2,1,0:T(8,128)S(1)}, f32[2,16,32,128]{3,2,1,0:T(8,128)S(1)}, u32[]{:S(2)}, u32[]{:S(2)}) collective-permute-start(f32[2,16,32,128]{3,2,1,0:T(8,128)S(1)} %get-tuple-element.18), channel_id=1, source_target_pairs={{0,8},{8,0},{16,24},{24,16},{1,9},{9,1},{17,25},{25,17},{2,10},{10... | collective-permute-start | bytes 1572872 | tf_op jit(solution)/shard_map/ppermute | solution.py:273
  74.1 15.9 %copy-start.10 = (bf16[256,256]{1,0:T(8,128)(2,1)S(1)}, bf16[256,256]{1,0:T(8,128)(2,1)}, u32[]{:S(2)}) copy-start(bf16[256,256]{1,0:T(8,128)(2,1)} %constant.92.clone.il) | copy-start | bytes 393220
  74.1 15.9 %copy-start.11 = (bf16[256,256]{1,0:T(8,128)(2,1)S(1)}, bf16[256,256]{1,0:T(8,128)(2,1)}, u32[]{:S(2)}) copy-start(bf16[256,256]{1,0:T(8,128)(2,1)} %constant.91.clone.ih) | copy-start | bytes 393220
  74.1 15.9 %copy-start.12 = (bf16[256,256]{1,0:T(8,128)(2,1)S(1)}, bf16[256,256]{1,0:T(8,128)(2,1)}, u32[]{:S(2)}) copy-start(bf16[256,256]{1,0:T(8,128)(2,1)} %constant.90.clone.fl) | copy-start | bytes 393220
  74.1 16.0 %copy-start.13 = (bf16[256,256]{1,0:T(8,128)(2,1)S(1)}, bf16[256,256]{1,0:T(8,128)(2,1)}, u32[]{:S(2)}) copy-start(bf16[256,256]{1,0:T(8,128)(2,1)} %constant.89.clone.fh) | copy-start | bytes 393220
  84.3 46.6 %all-to-all-start = ((f32[8,2,14,16,128]{4,3,2,1,0:T(8,128)}), f32[8,2,14,16,128]{4,3,2,1,0:T(8,128)}, u32[]{:S(2)}, u32[]{:S(2)}) async-start(f32[8,2,14,16,128]{4,3,2,1,0:T(8,128)} %shard_map.193), calls=%async_computation | async-start | bytes 3670016 | tf_op jit(solution)/shard_map/all_to_all | solution.py:265
  130.9 46.4 %all-to-all-start.3 = ((f32[8,2,14,16,128]{4,3,2,1,0:T(8,128)}), f32[8,2,14,16,128]{4,3,2,1,0:T(8,128)S(1)}, u32[]{:S(2)}, u32[]{:S(2)}) async-start(f32[8,2,14,16,128]{4,3,2,1,0:T(8,128)} %copy-done.4), calls=%async_computation.3 | async-start | bytes 3670016 | tf_op jit(solution)/shard_map/all_to_all | solution.py:265
  139.2 43.2 %copy-start.6 = (bf16[256,256]{1,0:T(8,128)(2,1)S(1)}, bf16[256,256]{1,0:T(8,128)(2,1)}, u32[]{:S(2)}) copy-start(bf16[256,256]{1,0:T(8,128)(2,1)} %constant.96.clone.rl) | copy-start | bytes 393220
  139.2 43.2 %copy-start.7 = (bf16[256,256]{1,0:T(8,128)(2,1)S(1)}, bf16[256,256]{1,0:T(8,128)(2,1)}, u32[]{:S(2)}) copy-start(bf16[256,256]{1,0:T(8,128)(2,1)} %constant.95.clone.rh) | copy-start | bytes 393220
  139.2 43.2 %copy-start.8 = (bf16[256,256]{1,0:T(8,128)(2,1)S(1)}, bf16[256,256]{1,0:T(8,128)(2,1)}, u32[]{:S(2)}) copy-start(bf16[256,256]{1,0:T(8,128)(2,1)} %constant.94.clone.ll) | copy-start | bytes 393220
  139.2 43.2 %copy-start.9 = (bf16[256,256]{1,0:T(8,128)(2,1)S(1)}, bf16[256,256]{1,0:T(8,128)(2,1)}, u32[]{:S(2)}) copy-start(bf16[256,256]{1,0:T(8,128)(2,1)} %constant.93.clone.lh) | copy-start | bytes 393220
  178.6 46.5 %all-to-all-start.1 = ((f32[8,2,14,16,128]{4,3,2,1,0:T(8,128)}), f32[8,2,14,16,128]{4,3,2,1,0:T(8,128)S(1)}, u32[]{:S(2)}, u32[]{:S(2)}) async-start(f32[8,2,14,16,128]{4,3,2,1,0:T(8,128)} %copy-done.3), calls=%async_computation.1 | async-start | bytes 3670016 | tf_op jit(solution)/shard_map/all_to_all | solution.py:265
  189.4 41.9 %collective-permute-start.11 = (f32[2,16,32,128]{3,2,1,0:T(8,128)}, f32[2,16,32,128]{3,2,1,0:T(8,128)}, u32[]{:S(2)}, u32[]{:S(2)}) collective-permute-start(f32[2,16,32,128]{3,2,1,0:T(8,128)} %get-tuple-element.24), channel_id=1, source_target_pairs={{0,24},{8,16},{16,8},{24,0},{1,25},{9,17},{17,9},{25,1},{2,26},{10... | collective-permute-start | bytes 1572872 | tf_op jit(solution)/shard_map/ppermute | solution.py:273
  190.2 41.3 %collective-permute-start.10 = (f32[2,16,32,128]{3,2,1,0:T(8,128)}, f32[2,16,32,128]{3,2,1,0:T(8,128)}, u32[]{:S(2)}, u32[]{:S(2)}) collective-permute-start(f32[2,16,32,128]{3,2,1,0:T(8,128)} %get-tuple-element.25), channel_id=1, source_target_pairs={{0,16},{8,24},{16,0},{24,8},{1,17},{9,25},{17,1},{25,9},{2,18},{10... | collective-permute-start | bytes 1572872 | tf_op jit(solution)/shard_map/ppermute | solution.py:273
  191.0 40.5 %collective-permute-start.9 = (f32[2,16,32,128]{3,2,1,0:T(8,128)S(1)}, f32[2,16,32,128]{3,2,1,0:T(8,128)}, u32[]{:S(2)}, u32[]{:S(2)}) collective-permute-start(f32[2,16,32,128]{3,2,1,0:T(8,128)S(1)} %get-tuple-element.26), channel_id=1, source_target_pairs={{0,8},{8,0},{16,24},{24,16},{1,9},{9,1},{17,25},{25,17},{2,10},{10... | collective-permute-start | bytes 1572872 | tf_op jit(solution)/shard_map/ppermute | solution.py:273
  229.6 14.2 %collective-permute-start.8 = (f32[2,16,32,128]{3,2,1,0:T(8,128)S(1)}, f32[2,16,32,128]{3,2,1,0:T(8,128)S(1)}, u32[]{:S(2)}, u32[]{:S(2)}) collective-permute-start(f32[2,16,32,128]{3,2,1,0:T(8,128)S(1)} %get-tuple-element.28), channel_id=1, source_target_pairs={{0,24},{8,16},{16,8},{24,0},{1,25},{9,17},{17,9},{25,1},{2,26},{10... | collective-permute-start | bytes 1572872 | tf_op jit(solution)/shard_map/ppermute | solution.py:273
  229.7 25.3 %collective-permute-start.7 = (f32[2,16,32,128]{3,2,1,0:T(8,128)S(1)}, f32[2,16,32,128]{3,2,1,0:T(8,128)S(1)}, u32[]{:S(2)}, u32[]{:S(2)}) collective-permute-start(f32[2,16,32,128]{3,2,1,0:T(8,128)S(1)} %get-tuple-element.29), channel_id=1, source_target_pairs={{0,16},{8,24},{16,0},{24,8},{1,17},{9,25},{17,1},{25,9},{2,18},{10... | collective-permute-start | bytes 1572872 | tf_op jit(solution)/shard_map/ppermute | solution.py:273
  231.3 23.8 %collective-permute-start.6 = (f32[2,16,32,128]{3,2,1,0:T(8,128)S(1)}, f32[2,16,32,128]{3,2,1,0:T(8,128)S(1)}, u32[]{:S(2)}, u32[]{:S(2)}) collective-permute-start(f32[2,16,32,128]{3,2,1,0:T(8,128)S(1)} %get-tuple-element.30), channel_id=1, source_target_pairs={{0,8},{8,0},{16,24},{24,16},{1,9},{9,1},{17,25},{25,17},{2,10},{10... | collective-permute-start | bytes 1572872 | tf_op jit(solution)/shard_map/ppermute | solution.py:273
  (12 other events, 31.8 us)
